TPU v7x, 256 devices: a whole 4x4x8 slice. The times are simulated.
256 devices in a mesh: dp: 128 (over z_hi, x, y, core), query: 2 (over z_lo).
Axes of the slice: x: 4, y: 4, z: 8 (z_hi: 4, z_lo: 2; z = z_hi * 2 + z_lo), core: 2. Of those that a mesh axis runs over, the one named last changes fastest.
Arguments:
- hidden_acts: bfloat16 [16384, 4, 14336], P(('dp', 'query')), may hold values from -5 to 5
- out_grads: bfloat16 [16384, 4, 4096], P(('dp', 'query')), may hold values from -5 to 5
- loss_mask: int32 [16384, 4], P(('dp', 'query')), may hold values from 0 to 1, as said below
- proj_in: bfloat16 [32, 14336], replicated, may hold values from -0.046875 to 0.046875
- proj_out: bfloat16 [32, 4096], replicated, may hold values from -0.09375 to 0.09375
- queries: float32 [256, 1024], P('query'), may hold values from -0.3125 to 0.3125
Outputs:
- scores: float32 [16384, 256], P(('dp', 'query'))
Inputs may be any that keep to these rules, and one draw needn't show every extreme that they name: `loss_mask`: the first token of every sequence counts.
All inputs are finite; a program needn't handle non-finite values.
Results may differ from a plain program's by a relative error of at most 0.0007.
Values sent between devices are 32-bit elements; how exact they have to be, the bound alone decides.
No kernel may reach another device: no remote copies, remote signals or barrier semaphores. Data moves between devices by JAX's collectives and lax.ppermute only.
A program may use at most 128 MiB of HBM per device.

v0:
```python
import functools

import jax
import jax.numpy as jnp
import numpy as np
from jax import lax
from jax.sharding import Mesh
from jax.sharding import PartitionSpec as P

K = 1024
DP_QUERY = ("dp_0", "dp_1", "dp_2", "dp_3", "query")


def copy_for_each(shard, axis):
    peers = lax.axis_size(axis)
    return lax.all_to_all(
        jnp.broadcast_to(shard[None], (peers, *shard.shape)), axis, 0, 0, tiled=True
    )


def laid_out(tiles, dim):
    tiles = jnp.moveaxis(tiles, 0, dim)
    lengths = tiles.shape
    return tiles.reshape(*lengths[:dim], lengths[dim] * lengths[dim + 1], *lengths[dim + 2 :])


def gather_directly(shard, axis, dim):
    tiles = copy_for_each(shard, axis)
    return laid_out(tiles, dim)


def by_axis(shard, axes):
    return functools.reduce(lax.psum, axes, shard)


def damped_solve(factor, columns):
    halfway = jax.scipy.linalg.solve_triangular(factor, columns, lower=True)
    return jax.scipy.linalg.solve_triangular(factor, halfway, lower=True, trans=1)


def pack_upper(matrix):
    tile_rows, tile_cols = np.triu_indices(8)
    tile_size = matrix.shape[0] // 8
    blocks = matrix.reshape(8, tile_size, 8, tile_size).transpose(0, 2, 1, 3)
    return blocks[tile_rows, tile_cols]


def unpack_upper(packed):
    tile_rows, tile_cols = np.triu_indices(8)
    position = np.zeros((8, 8), dtype=np.int32)
    position[tile_rows, tile_cols] = np.arange(tile_rows.shape[0])
    position[tile_cols, tile_rows] = np.arange(tile_rows.shape[0])
    below_diag = np.arange(8)[:, None] > np.arange(8)[None, :]
    tile_size = packed.shape[1]
    blocks = packed[position.reshape(-1)].reshape(8, 8, tile_size, tile_size)
    blocks = jnp.where(below_diag[:, :, None, None], jnp.swapaxes(blocks, 2, 3), blocks)
    return blocks.transpose(0, 2, 1, 3).reshape(8 * tile_size, 8 * tile_size)


def summed_gram(sketch):
    gram = lax.dot_general(
        sketch, sketch, (((0,), (0,)), ((), ())), precision=lax.Precision.HIGHEST
    )
    payload = pack_upper(gram)
    summed = lax.psum(payload, DP_QUERY)
    summed = unpack_upper(summed)
    return summed


def on_device(hidden_acts, out_grads, loss_mask, proj_in, proj_out, queries):
    seq_count, seq_tokens, hidden_width = hidden_acts.shape
    model_width = out_grads.shape[2]
    gathered = gather_directly(queries, "query", 0)
    is_live = loss_mask.astype(jnp.float32)
    local_count = jnp.sum(is_live)
    act_proj = lax.dot_general(
        hidden_acts.reshape(-1, hidden_width),
        proj_in,
        (((1,), (1,)), ((), ())),
        preferred_element_type=jnp.float32,
    ).reshape(seq_count, seq_tokens, proj_in.shape[0])
    grad_proj = lax.dot_general(
        out_grads.reshape(-1, model_width),
        proj_out,
        (((1,), (1,)), ((), ())),
        preferred_element_type=jnp.float32,
    ).reshape(seq_count, seq_tokens, proj_out.shape[0])
    weighted = grad_proj * is_live[:, :, None]
    outer = jnp.einsum("stg,stx->sgx", weighted, act_proj, precision=lax.Precision.HIGHEST).reshape(
        seq_count, K
    )
    token_total = by_axis(local_count, DP_QUERY)
    sketch = outer / token_total
    fisher = summed_gram(sketch)
    damping = 0.1 * jnp.trace(fisher) / K
    system = fisher + damping * jnp.eye(K, dtype=jnp.float32)
    factor = jnp.linalg.cholesky(system)
    solved = damped_solve(factor, gathered.T)
    return jnp.dot(sketch, solved, precision=lax.Precision.HIGHEST)


def solution(mesh):
    finer = Mesh(
        mesh.devices.reshape(4, 4, 4, 2, mesh.shape["query"]),
        ("dp_0", "dp_1", "dp_2", "dp_3", "query"),
    )
    in_specs = (
        P(DP_QUERY, None, None),
        P(DP_QUERY, None, None),
        P(DP_QUERY, None),
        P(),
        P(),
        P("query", None),
    )
    out_specs = P(DP_QUERY, None)
    return jax.shard_map(
        on_device, mesh=finer, in_specs=in_specs, out_specs=out_specs, check_vma=False
    )
```

profile of v0, /device:TPU:1, one launch (start us, length us, event | category | flops | bytes accessed | tf_op | source)
XLA Modules:
  0.0 722.2 jit_solution(6681472832962339901)
XLA Ops:
  7.9 14.3 %psum.42 = f32[]{:T(128)} all-reduce(f32[]{:T(128)} %convert_reduce_fusion), channel_id=1, replica_groups=mesh['dp_0'=4,'dp_1'=4,'dp_2'=4,'dp_3'=2,'query'=2] {'dp_0'}, use_global_device_ids=true, to_apply=%region_1.0 | all-reduce | flops 1 | bytes 8 | tf_op jit(solution)/shard_map/psum | solution.py:33
  22.9 9.4 %psum.43 = f32[]{:T(128)} all-reduce(f32[]{:T(128)} %psum.42), channel_id=1, replica_groups=mesh['dp_0'=4,'dp_1'=4,'dp_2'=4,'dp_3'=2,'query'=2] {'dp_1'}, use_global_device_ids=true, to_apply=%region_2.0 | all-reduce | flops 1 | bytes 8 | tf_op jit(solution)/shard_map/psum | solution.py:33
  36.3 9.4 %psum.44 = f32[]{:T(128)} all-reduce(f32[]{:T(128)} %psum.43), channel_id=1, replica_groups=mesh['dp_0'=4,'dp_1'=4,'dp_2'=4,'dp_3'=2,'query'=2] {'dp_2'}, use_global_device_ids=true, to_apply=%region_3.0 | all-reduce | flops 1 | bytes 8 | tf_op jit(solution)/shard_map/psum | solution.py:33
  45.7 10.9 %fusion = f32[64,4,32]{0,2,1:T(8,128)S(1)} fusion(bf16[64,4,14336]{2,1,0:T(4,128)(2,1)} %param.13, bf16[32,14336]{1,0:T(8,128)(2,1)S(1)} %copy-done), kind=kOutput, calls=%fused_computation.4 | convolution fusion | flops 234881024 | bytes 8290304 | tf_op jit(solution)/shard_map/dot_general | solution.py:76
  56.7 9.2 %psum.45 = f32[]{:T(128)} all-reduce(f32[]{:T(128)} %psum.44), channel_id=1, replica_groups=mesh['dp_0'=4,'dp_1'=4,'dp_2'=4,'dp_3'=2,'query'=2] {'dp_3'}, use_global_device_ids=true, to_apply=%region_4.0 | all-reduce | flops 1 | bytes 8 | tf_op jit(solution)/shard_map/psum | solution.py:33
  66.0 4.6 psum.46
  73.8 5.0 convolution_bitcast_fusion
  78.7 4.6 gather_fusion
  88.2 251.4 %all-reduce.3.cloned.1.call-done = f32[36,128,128]{2,1,0:T(8,128)} async-done(((f32[36,128,128]{2,1,0:T(8,128)}), f32[36,128,128]{2,1,0:T(8,128)}) %all-reduce.3.cloned.1.call-update) | async-done | bytes 2359312 | tf_op jit(solution)/shard_map/psum | solution.py:65
  343.9 5.4 copy.40
  349.3 7.9 %fusion.3 = (f32[]{:T(128)}, f32[8,8,128,128]{2,0,3,1:T(8,128)}) fusion(s32[8,128]{1,0:T(8,128)S(1)} %multiply_add_fusion, f32[8,8,128,128]{2,0,3,1:T(8,128)} %copy.40, f32[8,8,128,128]{3,2,1,0:T(8,128)} %bitcast.172, pred[8,8]{0,1:T(8,128)(4,1)S(1)} %copy-done.7), kind=kLoop, calls=%fused_computation.11 | loop fusion | flops 4194303 | bytes 12587076 | tf_op jit(solution)/shard_map/jit(trace)/reduce_sum | solution.py:95
  357.8 5.2 bitcast_add_fusion
  363.0 5.7 copy.41
  368.7 5.0 fusion.2
  375.7 11.7 %cholesky.222 = f32[128,128]{1,0:T(8,128)S(1)} custom-call(f32[128,128]{1,0:T(8,128)S(1)} %cholesky.577), custom_call_target="Cholesky" | custom-call | tf_op jit(solution)/shard_map/jit(cholesky)/cholesky | solution.py:97
  387.4 9.8 %custom-call.66 = f32[1,128,128]{1,2,0:T(8,128)S(1)} custom-call(f32[1,128,128]{2,1,0:T(8,128)S(1)} %get-tuple-element.63), custom_call_target="InvertDiagBlocksLowerTriangular" | custom-call | tf_op jit(solution)/shard_map/jit(cholesky)/cholesky | solution.py:97
  400.4 11.9 %cholesky.243 = f32[128,128]{1,0:T(8,128)S(1)} custom-call(f32[128,128]{1,0:T(8,128)S(1)} %cholesky.581), custom_call_target="Cholesky" | custom-call | tf_op jit(solution)/shard_map/jit(cholesky)/cholesky | solution.py:97
  412.7 9.8 %custom-call.67 = f32[1,128,128]{1,2,0:T(8,128)S(1)} custom-call(f32[1,128,128]{2,1,0:T(8,128)S(1)} %get-tuple-element.61), custom_call_target="InvertDiagBlocksLowerTriangular" | custom-call | tf_op jit(solution)/shard_map/jit(cholesky)/cholesky | solution.py:97
  428.0 11.7 %cholesky.466 = f32[128,128]{1,0:T(8,128)S(1)} custom-call(f32[128,128]{1,0:T(8,128)S(1)} %cholesky.586), custom_call_target="Cholesky" | custom-call | tf_op jit(solution)/shard_map/jit(cholesky)/cholesky | solution.py:97
  440.5 9.8 %custom-call.68 = f32[1,128,128]{1,2,0:T(8,128)S(1)} custom-call(f32[1,128,128]{2,1,0:T(8,128)S(1)} %get-tuple-element.59), custom_call_target="InvertDiagBlocksLowerTriangular" | custom-call | tf_op jit(solution)/shard_map/jit(cholesky)/cholesky | solution.py:97
  454.9 11.7 %cholesky.485 = f32[128,128]{1,0:T(8,128)S(1)} custom-call(f32[128,128]{1,0:T(8,128)S(1)} %cholesky.591), custom_call_target="Cholesky" | custom-call | tf_op jit(solution)/shard_map/jit(cholesky)/cholesky | solution.py:97
  467.4 9.8 %custom-call.69 = f32[1,128,128]{1,2,0:T(8,128)S(1)} custom-call(f32[1,128,128]{2,1,0:T(8,128)S(1)} %get-tuple-element.57), custom_call_target="InvertDiagBlocksLowerTriangular" | custom-call | tf_op jit(solution)/shard_map/jit(cholesky)/cholesky | solution.py:97
  481.5 12.1 %cholesky.504 = f32[128,128]{1,0:T(8,128)S(1)} custom-call(f32[128,128]{1,0:T(8,128)S(1)} %cholesky.596), custom_call_target="Cholesky" | custom-call | tf_op jit(solution)/shard_map/jit(cholesky)/cholesky | solution.py:97
  494.4 9.8 %custom-call.70 = f32[1,128,128]{1,2,0:T(8,128)S(1)} custom-call(f32[1,128,128]{2,1,0:T(8,128)S(1)} %get-tuple-element.55), custom_call_target="InvertDiagBlocksLowerTriangular" | custom-call | tf_op jit(solution)/shard_map/jit(cholesky)/cholesky | solution.py:97
  508.4 11.7 %cholesky.524 = f32[128,128]{1,0:T(8,128)S(1)} custom-call(f32[128,128]{1,0:T(8,128)S(1)} %cholesky.601), custom_call_target="Cholesky" | custom-call | tf_op jit(solution)/shard_map/jit(cholesky)/cholesky | solution.py:97
  520.9 9.8 %custom-call.71 = f32[1,128,128]{1,2,0:T(8,128)S(1)} custom-call(f32[1,128,128]{2,1,0:T(8,128)S(1)} %get-tuple-element.53), custom_call_target="InvertDiagBlocksLowerTriangular" | custom-call | tf_op jit(solution)/shard_map/jit(cholesky)/cholesky | solution.py:97
  534.6 11.7 %cholesky.544 = f32[128,128]{1,0:T(8,128)S(1)} custom-call(f32[128,128]{1,0:T(8,128)S(1)} %cholesky.606), custom_call_target="Cholesky" | custom-call | tf_op jit(solution)/shard_map/jit(cholesky)/cholesky | solution.py:97
  547.1 9.8 %custom-call.72 = f32[1,128,128]{1,2,0:T(8,128)S(1)} custom-call(f32[1,128,128]{2,1,0:T(8,128)S(1)} %get-tuple-element.51), custom_call_target="InvertDiagBlocksLowerTriangular" | custom-call | tf_op jit(solution)/shard_map/jit(cholesky)/cholesky | solution.py:97
  559.9 11.7 %cholesky.562 = f32[128,128]{1,0:T(8,128)S(1)} custom-call(f32[128,128]{1,0:T(8,128)S(1)} %convolution_subtract_fusion.20), custom_call_target="Cholesky" | custom-call | tf_op jit(solution)/shard_map/jit(cholesky)/cholesky | solution.py:97
  582.1 4.8 select_select_fusion
  586.9 28.5 %while.1 = (s32[]{:T(128)}, f32[1024,1024]{0,1:T(8,128)}, s32[8,2]{0,1:T(2,128)S(1)}, f32[8,128,128]{2,1,0:T(8,128)}, s32[]{:T(128)}) while((s32[]{:T(128)}, f32[1024,1024]{0,1:T(8,128)}, s32[8,2]{0,1:T(2,128)S(1)}, f32[8,128,128]{2,1,0:T(8,128)}, s32[]{:T(128)}) %tuple.51), condition=%wide.while_cond, body=%wide.while_body.sunk | while | flops 2 | bytes 393829 | solution.py:38
  615.4 79.6 %custom-call.73 = f32[8,128,128]{1,2,0:T(8,128)S(1)} custom-call(f32[8,128,128]{2,1,0:T(8,128)} %get-tuple-element.12), custom_call_target="InvertDiagBlocksLowerTriangular" | custom-call | tf_op jit(solution)/shard_map/jit(_solve_triangular)/triangular_solve | solution.py:38
  (184 shorter events, 106.7 us)
Async XLA Ops:
  6.5 39.2 %copy-start = (bf16[32,14336]{1,0:T(8,128)(2,1)S(1)}, bf16[32,14336]{1,0:T(8,128)(2,1)}, u32[]{:S(2)}) copy-start(bf16[32,14336]{1,0:T(8,128)(2,1)} %param.16) | copy-start | bytes 2752516
  6.5 333.0 %all-reduce.3.cloned.1.call-start = ((), (), s32[]{:S(2)}) async-start(), calls=%async_computation.1 | async-start | bytes 4718592 | tf_op jit(solution)/shard_map/psum | solution.py:65
  73.2 5.6 copy-start.5
  78.7 4.6 copy-start.6
  83.3 4.8 copy-start.8
  84.5 610.5 %all-to-all-start = ((f32[2,128,1024]{2,1,0:T(8,128)}), f32[2,128,1024]{2,1,0:T(8,128)S(1)}, u32[]{:S(2)}, u32[]{:S(2)}) async-start(f32[2,128,1024]{2,1,0:T(8,128)} %broadcast_in_dim.38), calls=%async_computation | async-start | bytes 2097152 | tf_op jit(solution)/shard_map/all_to_all | solution.py:16
  343.9 5.4 copy-start.7
  373.7 1.9 copy-start.4
  423.6 2.0 copy-start.2
  695.1 6.0 copy-start.3
  711.3 3.7 copy-start.1
Sparse Core Ops, SparseCore 0:
  83.5 256.0 all-reduce.2
where the time goes:
time: 732 us; the launch traced here: 722 us
  other arithmetic  273 us (37%)
  waiting for transfers between devices  251 us (34%)
  matrix products  67.4 us (9%)
  local copies, waits for them, and re-layouts  60.1 us (8%)
  blocking collectives  46.9 us (6%)
  between operations  20.2 us (3%)
    psum x1, waiting for transfers between devices, summed_gram(): summed = lax.psum(payload, DP_QUERY)  251 us
    another operation x30, other arithmetic, on_device(): factor = jnp.linalg.cholesky(system)  168 us
    another operation x3, other arithmetic, damped_solve(): jax.scipy.linalg.solve_triangular(factor, halfway, lower=True, trans=1)  84.4 us
    psum x5, blocking collectives, by_axis(): return functools.reduce(lax.psum, axes, shard)  46.9 us
    another operation x40, local copies, waits for them, and re-layouts  28.4 us
    another operation x14, matrix products, on_device(): factor = jnp.linalg.cholesky(system)  25.9 us
  transfers between devices with their start and end apart: 2, of which 1 were waited for; matrix products, arithmetic and copies ran while one was open for 48% of the time, Pallas kernels for 0%

commit v1 on v0

v1 whole, which is shorter than its diff:
```python
import functools

import jax
import jax.numpy as jnp
from jax import lax
from jax.experimental import pallas as pl
from jax.experimental.pallas import tpu as pltpu
from jax.sharding import Mesh
from jax.sharding import PartitionSpec as P

K = 1024
TILE = 128
SIDE = K // TILE
PACKED = SIDE * (SIDE + 1) // 2
AXES = ("z_hi", "x", "y", "core", "z_lo")
SIZES = {"z_hi": 4, "x": 4, "y": 4, "core": 2, "z_lo": 2}
STAGES = (("core",), ("x", "y"), ("z_hi", "z_lo"))
HI = lax.Precision.HIGHEST


def tile_index(i, j):
    return i * SIDE - i * (i - 1) // 2 + (j - i)


def dot_f32(a, b, dims):
    return lax.dot_general(a, b, (dims, ((), ())), precision=HI, preferred_element_type=jnp.float32)


def gram_body(act_ref, grad_ref, mask_ref, outer_ref, tiles_ref):
    live = mask_ref[...].astype(jnp.float32)
    tokens, width, seqs = act_ref.shape
    weighted = [grad_ref[t] * live[t : t + 1, :] for t in range(tokens)]
    acts = [act_ref[t] for t in range(tokens)]
    for g in range(K // width):
        total = weighted[0][g : g + 1, :] * acts[0]
        for t in range(1, tokens):
            total = total + weighted[t][g : g + 1, :] * acts[t]
        outer_ref[g * width : (g + 1) * width, :] = total
    for i in range(SIDE):
        rows = outer_ref[i * TILE : (i + 1) * TILE, :]
        strip = dot_f32(rows, outer_ref[i * TILE :, :], ((1,), (1,)))
        for j in range(i, SIDE):
            tiles_ref[tile_index(i, j)] = strip[:, (j - i) * TILE : (j - i + 1) * TILE]
    row = lax.broadcasted_iota(jnp.int32, (8, TILE), 0)
    lane = lax.broadcasted_iota(jnp.int32, (8, TILE), 1)
    count = jnp.sum(live)
    tiles_ref[0, 0:8, :] = jnp.where((row == 1) & (lane == 0), count, tiles_ref[0, 0:8, :])


def local_gram(act, grad, mask):
    seqs = act.shape[2]
    return pl.pallas_call(
        gram_body,
        out_shape=(
            jax.ShapeDtypeStruct((K, seqs), jnp.float32),
            jax.ShapeDtypeStruct((PACKED, TILE, TILE), jnp.float32),
        ),
        name="local_gram",
    )(act, grad, mask)


def invert_factor(src, dst):
    lane = lax.broadcasted_iota(jnp.int32, (8, TILE), 1)
    sub = lax.broadcasted_iota(jnp.int32, (8, TILE), 0)
    groups = TILE // 8
    for g in range(groups):
        tiles = [src[8 * q : 8 * q + 8, :] for q in range(g, groups)]
        cols = [
            [jnp.broadcast_to(t[:, 8 * g + j : 8 * g + j + 1], (8, TILE)) for t in tiles]
            for j in range(8)
        ]
        inside = (lane >= 8 * g) & (lane < 8 * g + 8)
        tiles = [jnp.where(inside, 0.0, t) for t in tiles]
        tiles[0] = jnp.where(lane == sub + 8 * g, 1.0, tiles[0])
        scale = jnp.zeros((8, TILE), jnp.float32)
        for j in range(8):
            pivot = jnp.broadcast_to(cols[j][0][j : j + 1, :], (8, TILE))
            inverse = 1.0 / pivot
            row = jnp.broadcast_to(tiles[0][j : j + 1, :], (8, TILE))
            root = lax.rsqrt(pivot)
            root = root * (1.5 - 0.5 * (pivot * root) * root)
            scale = jnp.where(sub == j, root, scale)
            factors = [c * inverse for c in cols[j]]
            factors[0] = jnp.where(sub > j, factors[0], 0.0)
            for l in range(j + 1, 8):
                top = jnp.broadcast_to(cols[l][0][j : j + 1, :], (8, TILE))
                cols[l] = [c - m * top for c, m in zip(cols[l], factors)]
            tiles = [t - m * row for t, m in zip(tiles, factors)]
        dst[8 * g : 8 * g + 8, :] = jnp.where(lane <= sub + 8 * g, tiles[0] * scale, 0.0)
        for q in range(1, len(tiles)):
            src[8 * (g + q) : 8 * (g + q) + 8, :] = tiles[q]


def solve_body(tiles_ref, query_ref, outer_ref, out_ref, a_ref, t_ref, l_ref, b_ref):
    queries = query_ref.shape[1]
    a_ref[...] = tiles_ref[...]
    b_ref[:, :queries] = query_ref[...]
    b_ref[:, queries:] = outer_ref[...]
    row = lax.broadcasted_iota(jnp.int32, (TILE, TILE), 0)
    lane = lax.broadcasted_iota(jnp.int32, (TILE, TILE), 1)
    eye = row == lane
    first = a_ref[0]
    holds_count = (row == 1) & (lane == 0)
    token_total = jnp.sum(jnp.where(holds_count, first, 0.0))
    twin = jnp.sum(jnp.where((row == 0) & (lane == 1), first, 0.0))
    a_ref[0] = jnp.where(holds_count, twin, first)
    trace = jnp.zeros((8, TILE), jnp.float32)
    for i in range(SIDE):
        diagonal = jnp.where(eye, a_ref[tile_index(i, i)], 0.0)
        trace = trace + jnp.sum(diagonal.reshape(TILE // 8, 8, TILE), axis=0)
    damping = 0.1 * jnp.sum(trace) / K
    for i in range(SIDE):
        a_ref[tile_index(i, i)] = a_ref[tile_index(i, i)] + jnp.where(eye, damping, 0.0)
    out_ref[...] = jnp.zeros_like(out_ref)

    def eliminate(k):
        inv = l_ref[...]
        rows = {j: dot_f32(inv, a_ref[tile_index(k, j)], ((1,), (0,))) for j in range(k + 1, SIDE)}
        right = dot_f32(inv, b_ref[TILE * k : TILE * (k + 1), :], ((1,), (0,)))
        for j in range(k + 1, SIDE):
            for c in range(j, SIDE):
                a_ref[tile_index(j, c)] -= dot_f32(rows[j], rows[c], ((0,), (0,)))
            b_ref[TILE * j : TILE * (j + 1), :] -= dot_f32(rows[j], right, ((0,), (0,)))
        out_ref[...] += dot_f32(right[:, queries:], right[:, :queries], ((0,), (0,)))

    def step(k, carry):
        t_ref[...] = a_ref[k * SIDE - (k * (k - 1)) // 2]
        invert_factor(t_ref, l_ref)
        for each in range(SIDE):
            pl.when(k == each)(functools.partial(eliminate, each))
        return carry

    lax.fori_loop(0, SIDE, step, 0)
    out_ref[...] = out_ref[...] * token_total


def damped_scores(tiles, queries_t, outer_t):
    queries, seqs = queries_t.shape[1], outer_t.shape[1]
    return pl.pallas_call(
        solve_body,
        out_shape=jax.ShapeDtypeStruct((seqs, queries), jnp.float32),
        scratch_shapes=[
            pltpu.VMEM((PACKED, TILE, TILE), jnp.float32),
            pltpu.VMEM((TILE, TILE), jnp.float32),
            pltpu.VMEM((TILE, TILE), jnp.float32),
            pltpu.VMEM((K, queries + seqs), jnp.float32),
        ],
        name="damped_scores",
    )(tiles, queries_t, outer_t)


def members(axes):
    count = 1
    for axis in axes:
        count *= SIZES[axis]
    return count


def scatter_sum(rows, axes):
    peers = members(axes)
    pieces = rows.reshape(peers, -1, TILE)
    return jnp.sum(lax.all_to_all(pieces, axes, 0, 0, tiled=True), axis=0)


def gather_rows(rows, axes):
    peers = members(axes)
    copies = jnp.broadcast_to(rows[None], (peers, *rows.shape))
    return lax.all_to_all(copies, axes, 0, 0, tiled=True).reshape(-1, TILE)


def summed(tiles):
    rows = tiles.reshape(-1, TILE)
    for axes in STAGES:
        rows = scatter_sum(rows, axes)
    for axes in reversed(STAGES):
        rows = gather_rows(rows, axes)
    return rows.reshape(tiles.shape)


def swap_queries(queries):
    other = lax.ppermute(queries, "z_lo", [(0, 1), (1, 0)])
    return jnp.concatenate([queries, other], axis=0).T


def on_device(hidden_acts, out_grads, loss_mask, proj_in, proj_out, queries):
    queries_t = swap_queries(queries)
    act = lax.dot_general(
        hidden_acts, proj_in, (((2,), (1,)), ((), ())), preferred_element_type=jnp.float32
    )
    grad = lax.dot_general(
        out_grads, proj_out, (((2,), (1,)), ((), ())), preferred_element_type=jnp.float32
    )
    outer_t, tiles = local_gram(act.transpose(1, 2, 0), grad.transpose(1, 2, 0), loss_mask.T)
    tiles = summed(tiles)
    scores = damped_scores(tiles, queries_t, outer_t)
    half = queries.shape[0]
    mine, other = scores[:, :half], scores[:, half:]
    is_first = lax.axis_index("z_lo") == 0
    return jnp.concatenate(
        [jnp.where(is_first, mine, other), jnp.where(is_first, other, mine)], axis=1
    )


def solution(mesh):
    finer = Mesh(mesh.devices.reshape(4, 4, 4, 2, mesh.shape["query"]), AXES)
    in_specs = (
        P(AXES, None, None),
        P(AXES, None, None),
        P(AXES, None),
        P(),
        P(),
        P("z_lo", None),
    )
    return jax.shard_map(
        on_device, mesh=finer, in_specs=in_specs, out_specs=P(AXES, None), check_vma=False
    )
```

time: 732 us -> 162 us (0.22); the launches traced: 722 us -> 162 us
  other arithmetic: 273 us -> 3.16 us
  waiting for transfers between devices: 251 us -> 12.4 us
  local copies, waits for them, and re-layouts: 60.1 us -> 3.26 us
  Pallas kernels: 0 us -> 54.2 us
  matrix products: 67.4 us -> 14.5 us
  blocking collectives: 46.9 us -> 70.2 us
  between operations: 20.2 us -> 0.08 us
    another operation x33 -> x0, other arithmetic: 252 us -> none  [the longest x30 168 us: on_device(): factor = jnp.linalg.cholesky(system)]
    psum x1 -> x0, waiting for transfers between devices: 251 us -> none  [summed_gram(): summed = lax.psum(payload, DP_QUERY)]
    all_to_all x0 -> x5, blocking collectives: none -> 70.2 us  [the longest x3 48.1 us: scatter_sum(): return jnp.sum(lax.all_to_all(pieces, axes, 0, 0, tiled=True), axis=0)]
    pallas_call x0 -> x2, Pallas kernels: none -> 54.2 us  [the longest x1 49.3 us: damped_scores(): pl.pallas_call(solve_body, out_shape=jax.ShapeDtypeStruct((seqs, queries)...]
    psum x5 -> x0, blocking collectives: 46.9 us -> none  [by_axis(): return functools.reduce(lax.psum, axes, shard)]
    another operation x44 -> x0, matrix products: 43.4 us -> none  [the longest x14 25.9 us: on_device(): factor = jnp.linalg.cholesky(system)]
    another operation x70 -> x0, local copies, waits for them, and re-layouts: 33.8 us -> none
    dot_general x5 -> x2, matrix products: 24 us -> 14.5 us  [the longest x1 11.5 us: on_device(): lax.dot_general(hidden_acts, proj_in, (((2,), (1,)), ((), ())), preferred...]
  transfers between devices with their start and end apart: 2 -> 2, of which waited for: 1 -> 2; matrix products, arithmetic and copies ran while one was open for 48% -> 1% of each run, Pallas kernels for 0% -> 0%
where the time goes in v1:
time: 162 us
  blocking collectives  70.2 us (43%)
  Pallas kernels  54.2 us (33%)
  matrix products  14.5 us (9%)
  waiting for transfers between devices  12.4 us (8%)
  starting transfers between devices  3.98 us (2%)
  local copies, waits for them, and re-layouts  3.26 us (2%)
  other arithmetic  3.16 us (2%)
    pallas_call x1, Pallas kernels, damped_scores(): pl.pallas_call(solve_body, out_shape=jax.ShapeDtypeStruct((seqs, queries)...  49.3 us
    all_to_all x3, blocking collectives, scatter_sum(): return jnp.sum(lax.all_to_all(pieces, axes, 0, 0, tiled=True), axis=0)  48.1 us
    all_to_all x2, blocking collectives, gather_rows(): return lax.all_to_all(copies, axes, 0, 0, tiled=True).reshape(-1, TILE)  22.1 us
    dot_general x1, matrix products, on_device(): lax.dot_general(hidden_acts, proj_in, (((2,), (1,)), ((), ())), preferred...  11.5 us
    ppermute x1, waiting for transfers between devices, swap_queries(): other = lax.ppermute(queries, 'z_lo', [(0, 1), (1, 0)])  9.19 us
    pallas_call x1, Pallas kernels, local_gram(): pl.pallas_call(gram_body, out_shape=(jax.ShapeDtypeStruct((K, seqs), jnp....  4.93 us
    all_to_all x1, starting transfers between devices, gather_rows(): return lax.all_to_all(copies, axes, 0, 0, tiled=True).reshape(-1, TILE)  3.7 us
  transfers between devices with their start and end apart: 2, of which 2 were waited for; matrix products, arithmetic and copies ran while one was open for 1% of the time, Pallas kernels for 0%

profile of v1, /device:TPU:1, one launch (start us, length us, event | category | flops | bytes accessed | tf_op | source)
XLA Modules:
  0.0 161.7 jit_solution(4331802645366484231)
XLA Ops:
  0.0 0.0 copy-start
  0.0 0.0 copy-start.2
  0.0 0.0 copy-start.3
  0.0 1.2 copy-done
  1.2 11.5 %fusion.4.act_ref = f32[4,32,64]{2,1,0:T(8,128)} fusion(bf16[64,4,14336]{2,1,0:T(4,128)(2,1)} %param.6, bf16[32,14336]{1,0:T(8,128)(2,1)S(1)} %copy-done), kind=kOutput, calls=%fused_computation.4 | convolution fusion | flops 234881024 | bytes 8290304 | tf_op jit(solution)/shard_map/dot_general | solution.py:187
  12.7 0.0 copy-done.2
  12.7 0.0 copy-done.3
  12.7 2.9 %fusion.7.grad_ref = f32[4,32,64]{2,1,0:T(8,128)} fusion(bf16[64,4,4096]{2,1,0:T(4,128)(2,1)S(1)} %copy-done.2, bf16[32,4096]{1,0:T(8,128)(2,1)S(1)} %copy-done.3), kind=kOutput, calls=%fused_computation.5 | convolution fusion | flops 67108864 | bytes 2392064 | tf_op jit(solution)/shard_map/dot_general | solution.py:190
  15.6 4.9 %local_gram.1 = (f32[1024,64]{1,0:T(8,128)}, f32[36,128,128]{2,1,0:T(8,128)}) custom-call(f32[4,32,64]{2,1,0:T(8,128)} %fusion.4.act_ref, f32[4,32,64]{2,1,0:T(8,128)} %fusion.7.grad_ref, s32[4,64]{1,0:T(4,128)} %bitcast.21), custom_call_target="tpu_custom_call" | custom-call | tf_op jit(solution)/shard_map/local_gram/pallas_call | solution.py:52
  20.6 9.7 %all_to_all.30 = f32[2,2304,128]{2,1,0:T(8,128)S(1)} all-to-all(f32[2,2304,128]{2,1,0:T(8,128)} %bitcast.20), channel_id=1, replica_groups=mesh['z_hi'=4,'x'=4,'y'=4,'core'=2,'z_lo'=2] {'core'}, dimensions={0} | all-to-all | bytes 4718592 | tf_op jit(solution)/shard_map/all_to_all | solution.py:162
  30.2 1.3 reduce_sum.27
  31.5 22.6 %all_to_all.31 = f32[16,144,128]{2,1,0:T(8,128)S(1)} all-to-all(f32[16,144,128]{2,1,0:T(8,128)} %bitcast.19), channel_id=1, replica_groups=mesh['z_hi'=4,'x'=4,'y'=4,'core'=2,'z_lo'=2] {'x','y'}, dimensions={0} | all-to-all | bytes 2359296 | tf_op jit(solution)/shard_map/all_to_all | solution.py:162
  54.2 0.1 reduce_sum.28
  54.2 0.0 copy-start.1
  54.3 15.8 %all_to_all.32 = f32[8,18,128]{2,1,0:T(8,128)S(1)} all-to-all(f32[8,18,128]{2,1,0:T(8,128)S(1)} %reshape.10), channel_id=1, replica_groups=mesh['z_hi'=4,'x'=4,'y'=4,'core'=2,'z_lo'=2] {'z_hi','z_lo'}, dimensions={0} | all-to-all | bytes 147456 | tf_op jit(solution)/shard_map/all_to_all | solution.py:162
  70.1 10.1 %all_to_all.33 = f32[8,18,128]{2,1,0:T(8,128)S(1)} all-to-all(f32[8,18,128]{2,1,0:T(8,128)S(1)} %broadcast_in_dim.20), channel_id=1, replica_groups=mesh['z_hi'=4,'x'=4,'y'=4,'core'=2,'z_lo'=2] {'z_hi','z_lo'}, dimensions={0} | all-to-all | bytes 147456 | tf_op jit(solution)/shard_map/all_to_all | solution.py:168
  80.2 1.1 broadcast_in_dim.22
  81.2 3.7 %all-to-all-start.4 = ((f32[16,144,128]{2,1,0:T(8,128)}), f32[16,144,128]{2,1,0:T(8,128)S(1)}, u32[]{:S(2)}, u32[]{:S(2)}) async-start(f32[16,144,128]{2,1,0:T(8,128)} %broadcast_in_dim.22), calls=%async_computation.4 | async-start | bytes 2359296 | tf_op jit(solution)/shard_map/all_to_all | solution.py:168
  84.9 0.0 copy-done.1
  85.0 0.2 copy.18
  85.2 0.3 collective-permute-start
  85.4 9.2 %collective-permute-done = f32[128,1024]{0,1:T(8,128)S(1)} collective-permute-done((f32[128,1024]{0,1:T(8,128)S(1)}, f32[128,1024]{0,1:T(8,128)S(1)}, u32[]{:S(2)}, u32[]{:S(2)}) %collective-permute-start) | collective-permute-done | bytes 524320 | tf_op jit(solution)/shard_map/ppermute | solution.py:181
  94.6 1.0 maximum_bitcast_fusion.query_ref
  95.7 3.2 %all-to-all-done.4 = f32[16,144,128]{2,1,0:T(8,128)S(1)} async-done(((f32[16,144,128]{2,1,0:T(8,128)}), f32[16,144,128]{2,1,0:T(8,128)S(1)}, u32[]{:S(2)}, u32[]{:S(2)}) %all-to-all-start.4) | async-done | bytes 1179680 | tf_op jit(solution)/shard_map/all_to_all | solution.py:168
  98.8 0.2 broadcast_in_dim.24
  99.0 12.1 %all_to_all.34 = f32[2,2304,128]{2,1,0:T(8,128)} all-to-all(f32[2,2304,128]{2,1,0:T(8,128)S(1)} %broadcast_in_dim.24), channel_id=1, replica_groups=mesh['z_hi'=4,'x'=4,'y'=4,'core'=2,'z_lo'=2] {'core'}, dimensions={0} | all-to-all | bytes 4718592 | tf_op jit(solution)/shard_map/all_to_all | solution.py:168
  111.0 49.3 %damped_scores.1 = f32[64,256]{1,0:T(8,128)} custom-call(f32[36,128,128]{2,1,0:T(8,128)} %bitcast.17, f32[1024,256]{1,0:T(8,128)} %maximum_bitcast_fusion.query_ref, f32[1024,64]{1,0:T(8,128)} %get-tuple-element.8.outer_ref), custom_call_target="tpu_custom_call" | custom-call | tf_op jit(solution)/shard_map/damped_scores/pallas_call | solution.py:139
  160.3 0.8 slice_select_fusion.1
  161.1 0.0 copy-start.4
  161.1 0.6 copy-done.4
  (5 shorter events, 0.0 us)
Async XLA Ops:
  0.0 1.2 copy-start
  0.0 12.7 %copy-start.2 = (bf16[64,4,4096]{2,1,0:T(4,128)(2,1)S(1)}, bf16[64,4,4096]{2,1,0:T(4,128)(2,1)}, u32[]{:S(2)}) copy-start(bf16[64,4,4096]{2,1,0:T(4,128)(2,1)} %param.7) | copy-start | bytes 6291460
  0.0 12.7 %copy-start.3 = (bf16[32,4096]{1,0:T(8,128)(2,1)S(1)}, bf16[32,4096]{1,0:T(8,128)(2,1)}, u32[]{:S(2)}) copy-start(bf16[32,4096]{1,0:T(8,128)(2,1)} %param.10) | copy-start | bytes 786436
  54.2 30.7 %copy-start.1 = (f32[128,1024]{1,0:T(8,128)S(1)}, f32[128,1024]{1,0:T(8,128)}, u32[]{:S(2)}) copy-start(f32[128,1024]{1,0:T(8,128)} %param.11) | copy-start | bytes 1572868
  81.2 17.6 %all-to-all-start.4 = ((f32[16,144,128]{2,1,0:T(8,128)}), f32[16,144,128]{2,1,0:T(8,128)S(1)}, u32[]{:S(2)}, u32[]{:S(2)}) async-start(f32[16,144,128]{2,1,0:T(8,128)} %broadcast_in_dim.22), calls=%async_computation.4 | async-start | bytes 2359296 | tf_op jit(solution)/shard_map/all_to_all | solution.py:168
  85.2 9.5 %collective-permute-start = (f32[128,1024]{0,1:T(8,128)S(1)}, f32[128,1024]{0,1:T(8,128)S(1)}, u32[]{:S(2)}, u32[]{:S(2)}) collective-permute-start(f32[128,1024]{0,1:T(8,128)S(1)} %copy.18), channel_id=1, source_target_pairs={{0,1},{1,0},{2,3},{3,2},{4,5},{5,4},{6,7},{7,6},{8,9},{9,8},{10,11... | collective-permute-start | bytes 1572872 | tf_op jit(solution)/shard_map/ppermute | solution.py:181
  161.1 0.6 copy-start.4

commit v2 on v1

v2 whole, which is shorter than its diff:
```python
import functools

import jax
import jax.numpy as jnp
from jax import lax
from jax.experimental import pallas as pl
from jax.experimental.pallas import tpu as pltpu
from jax.sharding import Mesh
from jax.sharding import PartitionSpec as P

K = 1024
TILE = 128
SIDE = K // TILE
PACKED = SIDE * (SIDE + 1) // 2
HALF = PACKED // 2
STEPS = 4
AXES = ("z_hi", "x", "y", "core", "z_lo")
SIZES = {"z_hi": 4, "x": 4, "y": 4, "core": 2, "z_lo": 2}
STAGES = (("x", "y"), ("z_hi", "z_lo"))
SWAP = [(0, 1), (1, 0)]


def tile_index(i, j):
    return i * SIDE - i * (i - 1) // 2 + (j - i)


def thirds(x):
    hi = x.astype(jnp.bfloat16)
    rest = x - hi.astype(jnp.float32)
    mid = rest.astype(jnp.bfloat16)
    low = (rest - mid.astype(jnp.float32)).astype(jnp.bfloat16)
    return hi, mid, low


def left_parts(parts, axis):
    hi, mid, low = parts
    return jnp.concatenate([low, mid, hi, mid, hi, hi], axis=axis)


def right_parts(parts, axis):
    hi, mid, low = parts
    return jnp.concatenate([hi, mid, low, hi, mid, hi], axis=axis)


def multiply(a, b):
    return jnp.dot(a, b, preferred_element_type=jnp.float32)


def multiply_rows(a, b):
    return lax.dot_general(a, b, (((1,), (1,)), ((), ())), preferred_element_type=jnp.float32)


def project(x_ref, w_ref, seqs, tokens):
    width = w_ref.shape[0]
    fold = TILE * 2 // width
    blocks = w_ref.shape[1] // TILE
    rows = fold * tokens
    per_seq = blocks * tokens
    left = [
        jnp.concatenate([x_ref[per_seq * s + rows * h : per_seq * s + rows * (h + 1), :] for s in range(seqs)], axis=0)
        for h in range(blocks // fold)
    ]
    right = [
        jnp.concatenate([w_ref[:, TILE * (fold * h + c) : TILE * (fold * h + c + 1)] for c in range(fold)], axis=0)
        for h in range(blocks // fold)
    ]
    all_pairs = multiply_rows(jnp.concatenate(left, axis=1), jnp.concatenate(right, axis=1))
    row = lax.broadcasted_iota(jnp.int32, all_pairs.shape, 0)
    lane = lax.broadcasted_iota(jnp.int32, all_pairs.shape, 1)
    matched = jnp.where((row // tokens) % fold == lane // width, all_pairs, 0.0)
    return jnp.sum(matched.reshape(seqs, rows // 8, 8, fold * width), axis=1).reshape(seqs * 8, fold * width)


def by_token(partial, width, tokens):
    fold_lane = lax.broadcasted_iota(jnp.int32, (width, partial.shape[1]), 1)
    fold_row = lax.broadcasted_iota(jnp.int32, (width, partial.shape[1]), 0)
    fold = jnp.where(fold_lane % width == fold_row, 1.0, 0.0).astype(jnp.bfloat16)
    hi, mid, low = thirds(partial)
    folded = multiply_rows(
        jnp.concatenate([fold] * 3, axis=1), jnp.concatenate([low, mid, hi], axis=1)
    )
    row = lax.broadcasted_iota(jnp.int32, (partial.shape[0], tokens * TILE), 0)
    lane = lax.broadcasted_iota(jnp.int32, (partial.shape[0], tokens * TILE), 1)
    pick = (row % tokens == lane // TILE) & (row // 8 == lane % TILE)
    pick = jnp.where(pick, 1.0, 0.0).astype(jnp.bfloat16)
    hi, mid, low = thirds(folded)
    return multiply(jnp.concatenate([low, mid, hi], axis=1), jnp.concatenate([pick] * 3, axis=0))


def gram_body(
    where_ref, act_ref, grad_ref, mask_ref, in_ref, out_ref, outer_ref, kept_ref, sent_ref, a_part, g_part, tiles
):
    tokens = mask_ref.shape[0]
    seqs = outer_ref.shape[1]
    some = seqs // STEPS
    step = pl.program_id(0)
    start = pl.multiple_of(step * some * 8, some * 8)
    a_part[pl.ds(start, some * 8), :] = project(act_ref, in_ref, some, tokens)
    g_part[pl.ds(start, some * 8), :] = project(grad_ref, out_ref, some, tokens)

    @pl.when(step == STEPS - 1)
    def _():
        live = mask_ref[...].astype(jnp.float32)
        width = in_ref.shape[0]
        acts = by_token(a_part[...], width, tokens)
        grads = by_token(g_part[...], out_ref.shape[0], tokens)
        acts = [acts[:, TILE * t : TILE * t + seqs] for t in range(tokens)]
        grads = [grads[:, TILE * t : TILE * t + seqs] * live[t : t + 1, :] for t in range(tokens)]
        for g in range(K // width):
            total = grads[0][g : g + 1, :] * acts[0]
            for t in range(1, tokens):
                total = total + grads[t][g : g + 1, :] * acts[t]
            outer_ref[g * width : (g + 1) * width, :] = total
        parts = thirds(outer_ref[...])
        left, right = left_parts(parts, 1), right_parts(parts, 1)
        for i in range(SIDE):
            strip = multiply_rows(left[TILE * i : TILE * (i + 1), :], right[TILE * i :, :])
            for j in range(i, SIDE):
                tiles[tile_index(i, j)] = strip[:, (j - i) * TILE : (j - i + 1) * TILE]
        row = lax.broadcasted_iota(jnp.int32, (8, TILE), 0)
        lane = lax.broadcasted_iota(jnp.int32, (8, TILE), 1)
        count = jnp.sum(live)
        tiles[0, 0:8, :] = jnp.where((row == 1) & (lane == 0), count, tiles[0, 0:8, :])
        core = where_ref[0]
        kept_ref[...] = tiles[pl.ds(core * HALF, HALF)]
        sent_ref[...] = tiles[pl.ds((1 - core) * HALF, HALF)]


def as_blocks(x):
    seqs, tokens, width = x.shape
    blocks = width // TILE
    return x.reshape(seqs, tokens, blocks, TILE).transpose(0, 2, 1, 3).reshape(seqs * blocks * tokens, TILE)


def local_gram(where, hidden_acts, out_grads, mask_t, proj_in, proj_out):
    seqs = hidden_acts.shape[0]
    acts, grads = as_blocks(hidden_acts), as_blocks(out_grads)

    def whole(shape):
        return pl.BlockSpec(shape, lambda i: (0,) * len(shape))

    half = (HALF, TILE, TILE)
    return pl.pallas_call(
        gram_body,
        grid=(STEPS,),
        in_specs=[
            pl.BlockSpec(memory_space=pltpu.SMEM),
            pl.BlockSpec((acts.shape[0] // STEPS, TILE), lambda i: (i, 0)),
            pl.BlockSpec((grads.shape[0] // STEPS, TILE), lambda i: (i, 0)),
            whole(mask_t.shape),
            whole(proj_in.shape),
            whole(proj_out.shape),
        ],
        out_specs=(whole((K, seqs)), whole(half), whole(half)),
        out_shape=(
            jax.ShapeDtypeStruct((K, seqs), jnp.float32),
            jax.ShapeDtypeStruct(half, jnp.float32),
            jax.ShapeDtypeStruct(half, jnp.float32),
        ),
        scratch_shapes=[
            pltpu.VMEM((seqs * 8, 2 * TILE), jnp.float32),
            pltpu.VMEM((seqs * 8, 2 * TILE), jnp.float32),
            pltpu.VMEM((PACKED, TILE, TILE), jnp.float32),
        ],
        name="local_gram",
    )(where, acts, grads, mask_t, proj_in, proj_out)


def invert_factor(src, dst):
    lane = lax.broadcasted_iota(jnp.int32, (8, TILE), 1)
    sub = lax.broadcasted_iota(jnp.int32, (8, TILE), 0)
    groups = TILE // 8
    for g in range(groups):
        tiles = [src[8 * q : 8 * q + 8, :] for q in range(g, groups)]
        cols = [
            [jnp.broadcast_to(t[:, 8 * g + j : 8 * g + j + 1], (8, TILE)) for t in tiles]
            for j in range(8)
        ]
        inside = (lane >= 8 * g) & (lane < 8 * g + 8)
        tiles = [jnp.where(inside, 0.0, t) for t in tiles]
        tiles[0] = jnp.where(lane == sub + 8 * g, 1.0, tiles[0])
        scale = jnp.zeros((8, TILE), jnp.float32)
        for j in range(8):
            pivot = jnp.broadcast_to(cols[j][0][j : j + 1, :], (8, TILE))
            guess = pl.reciprocal(pivot, approx=True)
            fix = 2.0 - pivot * guess
            inverse = guess * fix
            row = jnp.broadcast_to(tiles[0][j : j + 1, :], (8, TILE))
            root = lax.rsqrt(pivot)
            root = root * (1.5 - 0.5 * (pivot * root) * root)
            scale = jnp.where(sub == j, root, scale)
            lead = jnp.where(sub > j, cols[j][0] * guess, 0.0) * fix
            factors = [lead] + [c * inverse for c in cols[j][1:]]
            for l in range(j + 1, 8):
                top = jnp.broadcast_to(cols[l][0][j : j + 1, :], (8, TILE))
                cols[l] = [c - m * top for c, m in zip(cols[l], factors)]
            tiles = [t - m * row for t, m in zip(tiles, factors)]
        dst[8 * g : 8 * g + 8, :] = jnp.where(lane <= sub + 8 * g, tiles[0] * scale, 0.0)
        for q in range(1, len(tiles)):
            src[8 * (g + q) : 8 * (g + q) + 8, :] = tiles[q]


def solve_body(
    where_ref, mine_ref, other_ref, query_ref, query2_ref, outer_ref, out_ref, a_ref, t_ref, l_ref, b_ref
):
    half = query_ref.shape[0]
    queries = 2 * half
    core = where_ref[0]
    a_ref[pl.ds(core * HALF, HALF)] = mine_ref[...]
    a_ref[pl.ds((1 - core) * HALF, HALF)] = other_ref[...]
    b_ref[:, :half] = query_ref[...].T
    b_ref[:, half:queries] = query2_ref[...].T
    b_ref[:, queries:] = outer_ref[...]
    row = lax.broadcasted_iota(jnp.int32, (TILE, TILE), 0)
    lane = lax.broadcasted_iota(jnp.int32, (TILE, TILE), 1)
    eye = row == lane
    first = a_ref[0]
    holds_count = (row == 1) & (lane == 0)
    token_total = jnp.sum(jnp.where(holds_count, first, 0.0))
    twin = jnp.sum(jnp.where((row == 0) & (lane == 1), first, 0.0))
    a_ref[0] = jnp.where(holds_count, twin, first)
    trace = jnp.zeros((8, TILE), jnp.float32)
    for i in range(SIDE):
        diagonal = jnp.where(eye, a_ref[tile_index(i, i)], 0.0)
        trace = trace + jnp.sum(diagonal.reshape(TILE // 8, 8, TILE), axis=0)
    damping = 0.1 * jnp.sum(trace) / K
    for i in range(SIDE):
        a_ref[tile_index(i, i)] = a_ref[tile_index(i, i)] + jnp.where(eye, damping, 0.0)
    out_ref[...] = jnp.zeros_like(out_ref)

    def eliminate(k):
        right_of = [a_ref[tile_index(k, j)] for j in range(k + 1, SIDE)]
        strip = jnp.concatenate(right_of + [b_ref[TILE * k : TILE * (k + 1), :]], axis=1)
        strip = multiply(left_parts(thirds(l_ref[...]), 1), right_parts(thirds(strip), 0))
        wide = right_parts(thirds(strip), 0)
        width = TILE * (SIDE - 1 - k)

        def flipped(start, stop):
            return left_parts(thirds(strip[:, start:stop].T), 1)

        for j in range(k + 1, SIDE):
            start = TILE * (j - k - 1)
            delta = multiply(flipped(start, start + TILE), wide[:, start:])
            for c in range(j, SIDE):
                a_ref[tile_index(j, c)] -= delta[:, TILE * (c - j) : TILE * (c - j + 1)]
            b_ref[TILE * j : TILE * (j + 1), :] -= delta[:, TILE * (SIDE - j) :]
        out_ref[...] += multiply(flipped(width + queries, strip.shape[1]), wide[:, width : width + queries])

    def step(k, carry):
        t_ref[...] = a_ref[k * SIDE - (k * (k - 1)) // 2]
        invert_factor(t_ref, l_ref)
        for each in range(SIDE):
            pl.when(k == each)(functools.partial(eliminate, each))
        return carry

    lax.fori_loop(0, SIDE, step, 0)
    scores = out_ref[...] * token_total
    is_first = where_ref[1] == 0
    out_ref[:, :half] = jnp.where(is_first, scores[:, :half], scores[:, half:])
    out_ref[:, half:] = jnp.where(is_first, scores[:, half:], scores[:, :half])


def damped_scores(where, mine, other, my_queries, other_queries, outer_t):
    queries, seqs = 2 * my_queries.shape[0], outer_t.shape[1]
    vmem = pl.BlockSpec(memory_space=pltpu.VMEM)
    return pl.pallas_call(
        solve_body,
        in_specs=[pl.BlockSpec(memory_space=pltpu.SMEM), vmem, vmem, vmem, vmem, vmem],
        out_shape=jax.ShapeDtypeStruct((seqs, queries), jnp.float32),
        scratch_shapes=[
            pltpu.VMEM((PACKED, TILE, TILE), jnp.float32),
            pltpu.VMEM((TILE, TILE), jnp.float32),
            pltpu.VMEM((TILE, TILE), jnp.float32),
            pltpu.VMEM((K, queries + seqs), jnp.float32),
        ],
        name="damped_scores",
    )(where, mine, other, my_queries, other_queries, outer_t)


def members(axes):
    count = 1
    for axis in axes:
        count *= SIZES[axis]
    return count


def scatter_sum(rows, axes):
    peers = members(axes)
    pieces = rows.reshape(peers, -1, TILE)
    return jnp.sum(lax.all_to_all(pieces, axes, 0, 0, tiled=True), axis=0)


def gather_rows(rows, axes):
    peers = members(axes)
    copies = jnp.broadcast_to(rows[None], (peers, *rows.shape))
    return lax.all_to_all(copies, axes, 0, 0, tiled=True).reshape(-1, TILE)


def summed(kept, sent):
    rows = (kept + lax.ppermute(sent, "core", SWAP)).reshape(-1, TILE)
    for axes in STAGES:
        rows = scatter_sum(rows, axes)
    for axes in reversed(STAGES):
        rows = gather_rows(rows, axes)
    mine = rows.reshape(kept.shape)
    return mine, lax.ppermute(mine, "core", SWAP)


def on_device(hidden_acts, out_grads, loss_mask, proj_in, proj_out, queries):
    where = jnp.stack([lax.axis_index("core"), lax.axis_index("z_lo")]).astype(jnp.int32)
    other_queries = lax.ppermute(queries, "z_lo", SWAP)
    outer_t, kept, sent = local_gram(where, hidden_acts, out_grads, loss_mask.T, proj_in, proj_out)
    other_queries, kept, sent = lax.optimization_barrier((other_queries, kept, sent))
    mine, other = summed(kept, sent)
    return damped_scores(where, mine, other, queries, other_queries, outer_t)


def solution(mesh):
    finer = Mesh(mesh.devices.reshape(4, 4, 4, 2, mesh.shape["query"]), AXES)
    in_specs = (
        P(AXES, None, None),
        P(AXES, None, None),
        P(AXES, None),
        P(),
        P(),
        P("z_lo", None),
    )
    return jax.shard_map(
        on_device, mesh=finer, in_specs=in_specs, out_specs=P(AXES, None), check_vma=False
    )
```

time: 162 us -> 141 us (0.87)
  matrix products: 14.5 us -> 0 us
  waiting for transfers between devices: 12.4 us -> 5.16 us
  starting transfers between devices: 3.98 us -> 9.49 us
  blocking collectives: 70.2 us -> 66.9 us
  local copies, waits for them, and re-layouts: 3.26 us -> 1.16 us
  Pallas kernels: 54.2 us -> 56.2 us
    dot_general x2 -> x0, matrix products: 14.5 us -> none  [the longest x1 11.5 us: on_device(): lax.dot_general(hidden_acts, proj_in, (((2,), (1,)), ((), ())), preferred...]
    ppermute x1 -> x3, starting transfers between devices: 0.28 us -> 9.49 us  [the longest x1 5.38 us: summed(): return (mine, lax.ppermute(mine, 'core', SWAP))]
    all_to_all x3 -> x2, blocking collectives: 48.1 us -> 39.6 us  [scatter_sum(): return jnp.sum(lax.all_to_all(pieces, axes, 0, 0, tiled=True), axis=0)]
    all_to_all x2, blocking collectives: 22.1 us -> 27.3 us  [gather_rows(): return lax.all_to_all(copies, axes, 0, 0, tiled=True).reshape(-1, TILE)]
    ppermute x1 -> x3, waiting for transfers between devices: 9.19 us -> 5.16 us  [the longest x1 2.68 us: summed(): rows = (kept + lax.ppermute(sent, 'core', SWAP)).reshape(-1, TILE)]
    all_to_all x1 -> x0, starting transfers between devices: 3.7 us -> none  [gather_rows(): return lax.all_to_all(copies, axes, 0, 0, tiled=True).reshape(-1, TILE)]
    all_to_all x1 -> x0, waiting for transfers between devices: 3.17 us -> none  [gather_rows(): return lax.all_to_all(copies, axes, 0, 0, tiled=True).reshape(-1, TILE)]
    pallas_call x2, Pallas kernels: 54.2 us -> 56.2 us  [the longest x1 45.5 us: damped_scores(): pl.pallas_call(solve_body, in_specs=[pl.BlockSpec(memory_space=pltpu.SMEM...]
  transfers between devices with their start and end apart: 2 -> 3, of which waited for: 2 -> 2; matrix products, arithmetic and copies ran while one was open for 1% -> 0% of each run, Pallas kernels for 0% -> 8%
where the time goes in v2:
time: 141 us
  blocking collectives  66.9 us (47%)
  Pallas kernels  56.2 us (40%)
  starting transfers between devices  9.49 us (7%)
  waiting for transfers between devices  5.16 us (4%)
  other arithmetic  2.17 us (2%)
    pallas_call x1, Pallas kernels, damped_scores(): pl.pallas_call(solve_body, in_specs=[pl.BlockSpec(memory_space=pltpu.SMEM...  45.5 us
    all_to_all x2, blocking collectives, scatter_sum(): return jnp.sum(lax.all_to_all(pieces, axes, 0, 0, tiled=True), axis=0)  39.6 us
    all_to_all x2, blocking collectives, gather_rows(): return lax.all_to_all(copies, axes, 0, 0, tiled=True).reshape(-1, TILE)  27.3 us
    pallas_call x1, Pallas kernels, local_gram(): pl.pallas_call(gram_body, grid=(STEPS,), in_specs=[pl.BlockSpec(memory_sp...  10.8 us
    ppermute x1, starting transfers between devices, summed(): return (mine, lax.ppermute(mine, 'core', SWAP))  5.38 us
  transfers between devices with their start and end apart: 3, of which 2 were waited for; matrix products, arithmetic and copies ran while one was open for 0% of the time, Pallas kernels for 8%

profile of v2, /device:TPU:1, one launch (start us, length us, event | category | flops | bytes accessed | tf_op | source)
XLA Modules:
  0.0 141.2 jit_solution(3501308527365864985)
XLA Ops:
  0.0 2.5 %collective-permute-start = (f32[128,1024]{1,0:T(8,128)}, f32[128,1024]{1,0:T(8,128)S(1)}, u32[]{:S(2)}, u32[]{:S(2)}) collective-permute-start(f32[128,1024]{1,0:T(8,128)} %query_ref.1), channel_id=1, source_target_pairs={{0,1},{1,0},{2,3},{3,2},{4,5},{5,4},{6,7},{7,6},{8,9},{9,8},{10,11... | collective-permute-start | bytes 1572872 | tf_op jit(solution)/shard_map/ppermute | solution.py:311
  2.5 0.7 pad_add_fusion.where_ref
  3.1 10.8 %local_gram.1 = (f32[1024,64]{1,0:T(8,128)}, f32[18,128,128]{2,1,0:T(8,128)}, f32[18,128,128]{2,1,0:T(8,128)}) custom-call(s32[2]{0:T(128)} %pad_add_fusion.where_ref, bf16[28672,128]{1,0:T(8,128)(2,1)} %bitcast.15, bf16[8192,128]{1,0:T(8,128)(2,1)} %bitcast.19, s32[4,64]{1,0:T(4,128)} %bitcast.20, bf16[32,14336]{1,0:T(8,128)(2,1)} %in_ref.1, ...), custom_call_target="tpu_custom_call" | custom-call | tf_op jit(solution)/shard_map/local_gram/pallas_call | solution.py:143
  13.9 0.0 collective-permute-done.query2_ref
  13.9 0.0 copy-start.2
  13.9 1.7 %collective-permute-start.1 = (f32[18,128,128]{2,1,0:T(8,128)}, f32[18,128,128]{2,1,0:T(8,128)S(1)}, u32[]{:S(2)}, u32[]{:S(2)}) collective-permute-start(f32[18,128,128]{2,1,0:T(8,128)} %get-tuple-element.14), channel_id=1, source_target_pairs={{0,2},{2,0},{1,3},{3,1},{4,6},{6,4},{5,7},{7,5},{8,10},{10,8},{9,1... | collective-permute-start | bytes 3538952 | tf_op jit(solution)/shard_map/ppermute | solution.py:300
  15.5 2.7 %collective-permute-done.1 = f32[18,128,128]{2,1,0:T(8,128)S(1)} collective-permute-done((f32[18,128,128]{2,1,0:T(8,128)}, f32[18,128,128]{2,1,0:T(8,128)S(1)}, u32[]{:S(2)}, u32[]{:S(2)}) %collective-permute-start.1) | collective-permute-done | bytes 1179680 | tf_op jit(solution)/shard_map/ppermute | solution.py:300
  18.2 1.4 %add.3 = f32[18,128,128]{2,1,0:T(8,128)S(1)} add(f32[18,128,128]{2,1,0:T(8,128)} %get-tuple-element.13, f32[18,128,128]{2,1,0:T(8,128)S(1)} %collective-permute-done.1) | non-fusion elementwise | flops 294912 | bytes 3538944 | tf_op jit(solution)/shard_map/add | solution.py:300
  19.7 0.0 copy-done.2
  19.7 24.2 %all_to_all.20 = f32[16,144,128]{2,1,0:T(8,128)S(1)} all-to-all(f32[16,144,128]{2,1,0:T(8,128)S(1)} %bitcast.16), channel_id=1, replica_groups=mesh['z_hi'=4,'x'=4,'y'=4,'core'=2,'z_lo'=2] {'x','y'}, dimensions={0} | all-to-all | bytes 2359296 | tf_op jit(solution)/shard_map/all_to_all | solution.py:290
  43.8 0.1 reduce_sum.18
  43.9 15.5 %all_to_all.21 = f32[8,18,128]{2,1,0:T(8,128)S(1)} all-to-all(f32[8,18,128]{2,1,0:T(8,128)S(1)} %reshape.21), channel_id=1, replica_groups=mesh['z_hi'=4,'x'=4,'y'=4,'core'=2,'z_lo'=2] {'z_hi','z_lo'}, dimensions={0} | all-to-all | bytes 147456 | tf_op jit(solution)/shard_map/all_to_all | solution.py:290
  59.4 10.1 %all_to_all.22 = f32[8,18,128]{2,1,0:T(8,128)S(1)} all-to-all(f32[8,18,128]{2,1,0:T(8,128)S(1)} %broadcast_in_dim.6), channel_id=1, replica_groups=mesh['z_hi'=4,'x'=4,'y'=4,'core'=2,'z_lo'=2] {'z_hi','z_lo'}, dimensions={0} | all-to-all | bytes 147456 | tf_op jit(solution)/shard_map/all_to_all | solution.py:296
  69.5 0.1 broadcast_in_dim.15
  69.6 17.2 %all_to_all.23 = f32[16,144,128]{2,1,0:T(8,128)S(1)} all-to-all(f32[16,144,128]{2,1,0:T(8,128)S(1)} %broadcast_in_dim.15), channel_id=1, replica_groups=mesh['z_hi'=4,'x'=4,'y'=4,'core'=2,'z_lo'=2] {'x','y'}, dimensions={0} | all-to-all | bytes 2359296 | tf_op jit(solution)/shard_map/all_to_all | solution.py:296
  86.8 0.0 copy-start
  86.8 5.4 %collective-permute-start.2 = (f32[18,128,128]{2,1,0:T(8,128)S(1)}, f32[18,128,128]{2,1,0:T(8,128)S(1)}, u32[]{:S(2)}, u32[]{:S(2)}) collective-permute-start(f32[18,128,128]{2,1,0:T(8,128)S(1)} %bitcast.17), channel_id=1, source_target_pairs={{0,2},{2,0},{1,3},{3,1},{4,6},{6,4},{5,7},{7,5},{8,10},{10,8},{9,1... | collective-permute-start | bytes 3538952 | tf_op jit(solution)/shard_map/ppermute | solution.py:306
  92.2 2.5 %collective-permute-done.2.other_ref = f32[18,128,128]{2,1,0:T(8,128)S(1)} collective-permute-done((f32[18,128,128]{2,1,0:T(8,128)S(1)}, f32[18,128,128]{2,1,0:T(8,128)S(1)}, u32[]{:S(2)}, u32[]{:S(2)}) %collective-permute-start.2) | collective-permute-done | bytes 1179680 | tf_op jit(solution)/shard_map/ppermute | solution.py:306
  94.7 0.0 copy-start.1
  94.7 0.0 copy-done
  94.7 1.1 copy-done.1
  95.7 45.5 %damped_scores.1 = f32[64,256]{1,0:T(8,128)} custom-call(s32[2]{0:T(128)} %pad_add_fusion.where_ref, f32[18,128,128]{2,1,0:T(8,128)} %bitcast.18, f32[18,128,128]{2,1,0:T(8,128)} %copy-done.1, f32[128,1024]{1,0:T(8,128)} %query_ref.1, f32[128,1024]{1,0:T(8,128)} %copy-done.2, f32[1024,64]{1,0:T(8,128)} %get-tuple-element.16.outer_ref), custom_call_target="tpu_custom_call" | custom-call | tf_op jit(solution)/shard_map/damped_scores/pallas_call | solution.py:266
  (4 shorter events, 0.0 us)
Async XLA Ops:
  0.0 13.9 %collective-permute-start = (f32[128,1024]{1,0:T(8,128)}, f32[128,1024]{1,0:T(8,128)S(1)}, u32[]{:S(2)}, u32[]{:S(2)}) collective-permute-start(f32[128,1024]{1,0:T(8,128)} %query_ref.1), channel_id=1, source_target_pairs={{0,1},{1,0},{2,3},{3,2},{4,5},{5,4},{6,7},{7,6},{8,9},{9,8},{10,11... | collective-permute-start | bytes 1572872 | tf_op jit(solution)/shard_map/ppermute | solution.py:311
  13.9 5.8 %copy-start.2 = (f32[128,1024]{1,0:T(8,128)}, f32[128,1024]{1,0:T(8,128)S(1)}, u32[]{:S(2)}) copy-start(f32[128,1024]{1,0:T(8,128)S(1)} %collective-permute-done.query2_ref) | copy-start | bytes 1572868
  13.9 4.3 %collective-permute-start.1 = (f32[18,128,128]{2,1,0:T(8,128)}, f32[18,128,128]{2,1,0:T(8,128)S(1)}, u32[]{:S(2)}, u32[]{:S(2)}) collective-permute-start(f32[18,128,128]{2,1,0:T(8,128)} %get-tuple-element.14), channel_id=1, source_target_pairs={{0,2},{2,0},{1,3},{3,1},{4,6},{6,4},{5,7},{7,5},{8,10},{10,8},{9,1... | collective-permute-start | bytes 3538952 | tf_op jit(solution)/shard_map/ppermute | solution.py:300
  86.8 7.9 %copy-start = (f32[16,144,128]{2,1,0:T(8,128)}, f32[16,144,128]{2,1,0:T(8,128)S(1)}, u32[]{:S(2)}) copy-start(f32[16,144,128]{2,1,0:T(8,128)S(1)} %all_to_all.23) | copy-start | bytes 3538948
  86.8 7.9 %collective-permute-start.2 = (f32[18,128,128]{2,1,0:T(8,128)S(1)}, f32[18,128,128]{2,1,0:T(8,128)S(1)}, u32[]{:S(2)}, u32[]{:S(2)}) collective-permute-start(f32[18,128,128]{2,1,0:T(8,128)S(1)} %bitcast.17), channel_id=1, source_target_pairs={{0,2},{2,0},{1,3},{3,1},{4,6},{6,4},{5,7},{7,5},{8,10},{10,8},{9,1... | collective-permute-start | bytes 3538952 | tf_op jit(solution)/shard_map/ppermute | solution.py:306
  94.7 1.1 copy-start.1

commit v3 on v2

--- a/solution.py
+++ b/solution.py
@@ -16,7 +16,7 @@
 STEPS = 4
 AXES = ("z_hi", "x", "y", "core", "z_lo")
 SIZES = {"z_hi": 4, "x": 4, "y": 4, "core": 2, "z_lo": 2}
-STAGES = (("x", "y"), ("z_hi", "z_lo"))
+NEAR = ("x", "y", "z_lo")
 SWAP = [(0, 1), (1, 0)]
 
 
@@ -88,7 +88,7 @@
 
 
 def gram_body(
-    where_ref, act_ref, grad_ref, mask_ref, in_ref, out_ref, outer_ref, kept_ref, sent_ref, a_part, g_part, tiles
+    act_ref, grad_ref, mask_ref, in_ref, out_ref, outer_ref, kept_ref, sent_ref, a_part, g_part, tiles
 ):
     tokens = mask_ref.shape[0]
     seqs = outer_ref.shape[1]
@@ -121,7 +121,7 @@
         lane = lax.broadcasted_iota(jnp.int32, (8, TILE), 1)
         count = jnp.sum(live)
         tiles[0, 0:8, :] = jnp.where((row == 1) & (lane == 0), count, tiles[0, 0:8, :])
-        core = where_ref[0]
+        core = lax.axis_index("core")
         kept_ref[...] = tiles[pl.ds(core * HALF, HALF)]
         sent_ref[...] = tiles[pl.ds((1 - core) * HALF, HALF)]
 
@@ -132,7 +132,7 @@
     return x.reshape(seqs, tokens, blocks, TILE).transpose(0, 2, 1, 3).reshape(seqs * blocks * tokens, TILE)
 
 
-def local_gram(where, hidden_acts, out_grads, mask_t, proj_in, proj_out):
+def local_gram(hidden_acts, out_grads, mask_t, proj_in, proj_out):
     seqs = hidden_acts.shape[0]
     acts, grads = as_blocks(hidden_acts), as_blocks(out_grads)
 
@@ -144,7 +144,6 @@
         gram_body,
         grid=(STEPS,),
         in_specs=[
-            pl.BlockSpec(memory_space=pltpu.SMEM),
             pl.BlockSpec((acts.shape[0] // STEPS, TILE), lambda i: (i, 0)),
             pl.BlockSpec((grads.shape[0] // STEPS, TILE), lambda i: (i, 0)),
             whole(mask_t.shape),
@@ -163,7 +162,7 @@
             pltpu.VMEM((PACKED, TILE, TILE), jnp.float32),
         ],
         name="local_gram",
-    )(where, acts, grads, mask_t, proj_in, proj_out)
+    )(acts, grads, mask_t, proj_in, proj_out)
 
 
 def invert_factor(src, dst):
@@ -201,11 +200,11 @@
 
 
 def solve_body(
-    where_ref, mine_ref, other_ref, query_ref, query2_ref, outer_ref, out_ref, a_ref, t_ref, l_ref, b_ref
+    mine_ref, other_ref, query_ref, query2_ref, outer_ref, out_ref, a_ref, t_ref, l_ref, b_ref
 ):
     half = query_ref.shape[0]
     queries = 2 * half
-    core = where_ref[0]
+    core = lax.axis_index("core")
     a_ref[pl.ds(core * HALF, HALF)] = mine_ref[...]
     a_ref[pl.ds((1 - core) * HALF, HALF)] = other_ref[...]
     b_ref[:, :half] = query_ref[...].T
@@ -255,17 +254,17 @@
 
     lax.fori_loop(0, SIDE, step, 0)
     scores = out_ref[...] * token_total
-    is_first = where_ref[1] == 0
+    is_first = lax.axis_index("z_lo") == 0
     out_ref[:, :half] = jnp.where(is_first, scores[:, :half], scores[:, half:])
     out_ref[:, half:] = jnp.where(is_first, scores[:, half:], scores[:, :half])
 
 
-def damped_scores(where, mine, other, my_queries, other_queries, outer_t):
+def damped_scores(mine, other, my_queries, other_queries, outer_t):
     queries, seqs = 2 * my_queries.shape[0], outer_t.shape[1]
     vmem = pl.BlockSpec(memory_space=pltpu.VMEM)
     return pl.pallas_call(
         solve_body,
-        in_specs=[pl.BlockSpec(memory_space=pltpu.SMEM), vmem, vmem, vmem, vmem, vmem],
+        in_specs=[vmem] * 5,
         out_shape=jax.ShapeDtypeStruct((seqs, queries), jnp.float32),
         scratch_shapes=[
             pltpu.VMEM((PACKED, TILE, TILE), jnp.float32),
@@ -274,7 +273,7 @@
             pltpu.VMEM((K, queries + seqs), jnp.float32),
         ],
         name="damped_scores",
-    )(where, mine, other, my_queries, other_queries, outer_t)
+    )(mine, other, my_queries, other_queries, outer_t)
 
 
 def members(axes):
@@ -298,21 +297,19 @@
 
 def summed(kept, sent):
     rows = (kept + lax.ppermute(sent, "core", SWAP)).reshape(-1, TILE)
-    for axes in STAGES:
-        rows = scatter_sum(rows, axes)
-    for axes in reversed(STAGES):
-        rows = gather_rows(rows, axes)
+    rows = scatter_sum(rows, NEAR)
+    everyone = gather_rows(rows, ("z_hi",)).reshape(SIZES["z_hi"], -1, TILE)
+    rows = gather_rows(jnp.sum(everyone, axis=0), NEAR)
     mine = rows.reshape(kept.shape)
     return mine, lax.ppermute(mine, "core", SWAP)
 
 
 def on_device(hidden_acts, out_grads, loss_mask, proj_in, proj_out, queries):
-    where = jnp.stack([lax.axis_index("core"), lax.axis_index("z_lo")]).astype(jnp.int32)
     other_queries = lax.ppermute(queries, "z_lo", SWAP)
-    outer_t, kept, sent = local_gram(where, hidden_acts, out_grads, loss_mask.T, proj_in, proj_out)
+    outer_t, kept, sent = local_gram(hidden_acts, out_grads, loss_mask.T, proj_in, proj_out)
     other_queries, kept, sent = lax.optimization_barrier((other_queries, kept, sent))
     mine, other = summed(kept, sent)
-    return damped_scores(where, mine, other, queries, other_queries, outer_t)
+    return damped_scores(mine, other, queries, other_queries, outer_t)
 
 
 def solution(mesh):

time: 141 us -> 134 us (0.950)
  blocking collectives: 66.9 us -> 61.5 us
    all_to_all x2 -> x1, blocking collectives: 39.6 us -> 26.5 us  [scatter_sum(): return jnp.sum(lax.all_to_all(pieces, axes, 0, 0, tiled=True), axis=0)]
    all_to_all x2, blocking collectives: 27.3 us -> 35 us  [gather_rows(): return lax.all_to_all(copies, axes, 0, 0, tiled=True).reshape(-1, TILE)]
    ppermute x1, starting transfers between devices: 5.38 us -> 3.6 us  [summed(): return (mine, lax.ppermute(mine, 'core', SWAP))]
where the time goes in v3:
time: 134 us
  blocking collectives  61.5 us (46%)
  Pallas kernels  56.3 us (42%)
  starting transfers between devices  8.22 us (6%)
  waiting for transfers between devices  5.2 us (4%)
  other arithmetic  1.51 us (1%)
    pallas_call x1, Pallas kernels, damped_scores(): pl.pallas_call(solve_body, in_specs=[vmem] * 5, out_shape=jax.ShapeDtypeS...  45.5 us
    all_to_all x2, blocking collectives, gather_rows(): return lax.all_to_all(copies, axes, 0, 0, tiled=True).reshape(-1, TILE)  35 us
    all_to_all x1, blocking collectives, scatter_sum(): return jnp.sum(lax.all_to_all(pieces, axes, 0, 0, tiled=True), axis=0)  26.5 us
    pallas_call x1, Pallas kernels, local_gram(): pl.pallas_call(gram_body, grid=(STEPS,), in_specs=[pl.BlockSpec((acts.sha...  10.9 us
    ppermute x1, starting transfers between devices, summed(): return (mine, lax.ppermute(mine, 'core', SWAP))  3.6 us
    ppermute x1, waiting for transfers between devices, summed(): rows = (kept + lax.ppermute(sent, 'core', SWAP)).reshape(-1, TILE)  2.68 us
  transfers between devices with their start and end apart: 3, of which 2 were waited for; matrix products, arithmetic and copies ran while one was open for 0% of the time, Pallas kernels for 8%

profile of v3, /device:TPU:1, one launch (start us, length us, event | category | flops | bytes accessed | tf_op | source)
XLA Modules:
  0.0 133.9 jit_solution(108759619710174899)
XLA Ops:
  0.0 2.5 %collective-permute-start = (f32[128,1024]{1,0:T(8,128)}, f32[128,1024]{1,0:T(8,128)S(1)}, u32[]{:S(2)}, u32[]{:S(2)}) collective-permute-start(f32[128,1024]{1,0:T(8,128)} %query_ref.1), channel_id=1, source_target_pairs={{0,1},{1,0},{2,3},{3,2},{4,5},{5,4},{6,7},{7,6},{8,9},{9,8},{10,11... | collective-permute-start | bytes 1572872 | tf_op jit(solution)/shard_map/ppermute | solution.py:308
  2.5 10.9 %local_gram.1 = (f32[1024,64]{1,0:T(8,128)}, f32[18,128,128]{2,1,0:T(8,128)}, f32[18,128,128]{2,1,0:T(8,128)}) custom-call(bf16[28672,128]{1,0:T(8,128)(2,1)} %bitcast.13, bf16[8192,128]{1,0:T(8,128)(2,1)} %bitcast.17, s32[4,64]{1,0:T(4,128)} %bitcast.18, bf16[32,14336]{1,0:T(8,128)(2,1)} %in_ref.1, bf16[32,4096]{1,0:T(8,128)(2,1)} %out_ref.1), custom_call_target="tpu_custom_call" | custom-call | tf_op jit(solution)/shard_map/local_gram/pallas_call | solution.py:143
  13.3 0.0 collective-permute-done.query2_ref
  13.4 0.0 copy-start.2
  13.4 2.2 %collective-permute-start.1 = (f32[18,128,128]{2,1,0:T(8,128)}, f32[18,128,128]{2,1,0:T(8,128)S(1)}, u32[]{:S(2)}, u32[]{:S(2)}) collective-permute-start(f32[18,128,128]{2,1,0:T(8,128)} %get-tuple-element.14), channel_id=1, source_target_pairs={{0,2},{2,0},{1,3},{3,1},{4,6},{6,4},{5,7},{7,5},{8,10},{10,8},{9,1... | collective-permute-start | bytes 3538952 | tf_op jit(solution)/shard_map/ppermute | solution.py:299
  15.5 2.7 %collective-permute-done.1 = f32[18,128,128]{2,1,0:T(8,128)S(1)} collective-permute-done((f32[18,128,128]{2,1,0:T(8,128)}, f32[18,128,128]{2,1,0:T(8,128)S(1)}, u32[]{:S(2)}, u32[]{:S(2)}) %collective-permute-start.1) | collective-permute-done | bytes 1179680 | tf_op jit(solution)/shard_map/ppermute | solution.py:299
  18.2 1.4 %add.3 = f32[18,128,128]{2,1,0:T(8,128)S(1)} add(f32[18,128,128]{2,1,0:T(8,128)} %get-tuple-element.13, f32[18,128,128]{2,1,0:T(8,128)S(1)} %collective-permute-done.1) | non-fusion elementwise | flops 294912 | bytes 3538944 | tf_op jit(solution)/shard_map/add | solution.py:299
  19.7 0.0 copy-done.2
  19.7 26.5 %all_to_all.15 = f32[32,72,128]{2,1,0:T(8,128)S(1)} all-to-all(f32[32,72,128]{2,1,0:T(8,128)S(1)} %bitcast.14), channel_id=1, replica_groups=mesh['z_hi'=4,'x'=4,'y'=4,'core'=2,'z_lo'=2] {'x','y','z_lo'}, dimensions={0} | all-to-all | bytes 2359296 | tf_op jit(solution)/shard_map/all_to_all | solution.py:289
  46.1 0.1 reduce_sum.18
  46.2 15.0 %all_to_all.16 = f32[4,72,128]{2,1,0:T(8,128)S(1)} all-to-all(f32[4,72,128]{2,1,0:T(8,128)S(1)} %broadcast_in_dim.4), channel_id=1, replica_groups=mesh['z_hi'=4,'x'=4,'y'=4,'core'=2,'z_lo'=2] {'z_hi'}, dimensions={0} | all-to-all | bytes 294912 | tf_op jit(solution)/shard_map/all_to_all | solution.py:295
  61.2 0.1 broadcast_in_dim.5
  61.3 20.1 %all_to_all.17 = f32[32,72,128]{2,1,0:T(8,128)S(1)} all-to-all(f32[32,72,128]{2,1,0:T(8,128)S(1)} %broadcast_in_dim.5), channel_id=1, replica_groups=mesh['z_hi'=4,'x'=4,'y'=4,'core'=2,'z_lo'=2] {'x','y','z_lo'}, dimensions={0} | all-to-all | bytes 2359296 | tf_op jit(solution)/shard_map/all_to_all | solution.py:295
  81.4 0.0 copy-start
  81.4 3.6 %collective-permute-start.2 = (f32[18,128,128]{2,1,0:T(8,128)S(1)}, f32[18,128,128]{2,1,0:T(8,128)S(1)}, u32[]{:S(2)}, u32[]{:S(2)}) collective-permute-start(f32[18,128,128]{2,1,0:T(8,128)S(1)} %bitcast.15), channel_id=1, source_target_pairs={{0,2},{2,0},{1,3},{3,1},{4,6},{6,4},{5,7},{7,5},{8,10},{10,8},{9,1... | collective-permute-start | bytes 3538952 | tf_op jit(solution)/shard_map/ppermute | solution.py:304
  85.0 2.5 %collective-permute-done.2.other_ref = f32[18,128,128]{2,1,0:T(8,128)S(1)} collective-permute-done((f32[18,128,128]{2,1,0:T(8,128)S(1)}, f32[18,128,128]{2,1,0:T(8,128)S(1)}, u32[]{:S(2)}, u32[]{:S(2)}) %collective-permute-start.2) | collective-permute-done | bytes 1179680 | tf_op jit(solution)/shard_map/ppermute | solution.py:304
  87.4 0.0 copy-start.1
  87.4 0.0 copy-done
  87.4 1.1 copy-done.1
  88.5 45.5 %damped_scores.1 = f32[64,256]{1,0:T(8,128)} custom-call(f32[18,128,128]{2,1,0:T(8,128)} %bitcast.16, f32[18,128,128]{2,1,0:T(8,128)} %copy-done.1, f32[128,1024]{1,0:T(8,128)} %query_ref.1, f32[128,1024]{1,0:T(8,128)} %copy-done.2, f32[1024,64]{1,0:T(8,128)} %get-tuple-element.16.outer_ref), custom_call_target="tpu_custom_call" | custom-call | tf_op jit(solution)/shard_map/damped_scores/pallas_call | solution.py:265
  (2 shorter events, 0.0 us)
Async XLA Ops:
  0.0 13.4 %collective-permute-start = (f32[128,1024]{1,0:T(8,128)}, f32[128,1024]{1,0:T(8,128)S(1)}, u32[]{:S(2)}, u32[]{:S(2)}) collective-permute-start(f32[128,1024]{1,0:T(8,128)} %query_ref.1), channel_id=1, source_target_pairs={{0,1},{1,0},{2,3},{3,2},{4,5},{5,4},{6,7},{7,6},{8,9},{9,8},{10,11... | collective-permute-start | bytes 1572872 | tf_op jit(solution)/shard_map/ppermute | solution.py:308
  13.4 6.3 %copy-start.2 = (f32[128,1024]{1,0:T(8,128)}, f32[128,1024]{1,0:T(8,128)S(1)}, u32[]{:S(2)}) copy-start(f32[128,1024]{1,0:T(8,128)S(1)} %collective-permute-done.query2_ref) | copy-start | bytes 1572868
  13.4 4.8 %collective-permute-start.1 = (f32[18,128,128]{2,1,0:T(8,128)}, f32[18,128,128]{2,1,0:T(8,128)S(1)}, u32[]{:S(2)}, u32[]{:S(2)}) collective-permute-start(f32[18,128,128]{2,1,0:T(8,128)} %get-tuple-element.14), channel_id=1, source_target_pairs={{0,2},{2,0},{1,3},{3,1},{4,6},{6,4},{5,7},{7,5},{8,10},{10,8},{9,1... | collective-permute-start | bytes 3538952 | tf_op jit(solution)/shard_map/ppermute | solution.py:299
  81.4 6.1 %copy-start = (f32[32,72,128]{2,1,0:T(8,128)}, f32[32,72,128]{2,1,0:T(8,128)S(1)}, u32[]{:S(2)}) copy-start(f32[32,72,128]{2,1,0:T(8,128)S(1)} %all_to_all.17) | copy-start | bytes 3538948
  81.4 6.1 %collective-permute-start.2 = (f32[18,128,128]{2,1,0:T(8,128)S(1)}, f32[18,128,128]{2,1,0:T(8,128)S(1)}, u32[]{:S(2)}, u32[]{:S(2)}) collective-permute-start(f32[18,128,128]{2,1,0:T(8,128)S(1)} %bitcast.15), channel_id=1, source_target_pairs={{0,2},{2,0},{1,3},{3,1},{4,6},{6,4},{5,7},{7,5},{8,10},{10,8},{9,1... | collective-permute-start | bytes 3538952 | tf_op jit(solution)/shard_map/ppermute | solution.py:304
  87.4 1.1 copy-start.1

commit v4 on v3

--- a/solution.py
+++ b/solution.py
@@ -71,20 +71,20 @@
     return jnp.sum(matched.reshape(seqs, rows // 8, 8, fold * width), axis=1).reshape(seqs * 8, fold * width)
 
 
-def by_token(partial, width, tokens):
-    fold_lane = lax.broadcasted_iota(jnp.int32, (width, partial.shape[1]), 1)
-    fold_row = lax.broadcasted_iota(jnp.int32, (width, partial.shape[1]), 0)
-    fold = jnp.where(fold_lane % width == fold_row, 1.0, 0.0).astype(jnp.bfloat16)
-    hi, mid, low = thirds(partial)
-    folded = multiply_rows(
-        jnp.concatenate([fold] * 3, axis=1), jnp.concatenate([low, mid, hi], axis=1)
-    )
-    row = lax.broadcasted_iota(jnp.int32, (partial.shape[0], tokens * TILE), 0)
-    lane = lax.broadcasted_iota(jnp.int32, (partial.shape[0], tokens * TILE), 1)
-    pick = (row % tokens == lane // TILE) & (row // 8 == lane % TILE)
-    pick = jnp.where(pick, 1.0, 0.0).astype(jnp.bfloat16)
-    hi, mid, low = thirds(folded)
-    return multiply(jnp.concatenate([low, mid, hi], axis=1), jnp.concatenate([pick] * 3, axis=0))
+def by_token(part_ref, width, token, tokens):
+    seqs = part_ref.shape[1] // 8
+
+    def picked(at):
+        return jnp.concatenate([part_ref[h, pl.ds(at, seqs, stride=8), :] for h in range(2)], axis=1)
+
+    rows = picked(token)
+    for other in range(token + tokens, 8, tokens):
+        rows = rows + picked(other)
+    row = lax.broadcasted_iota(jnp.int32, (width, rows.shape[1]), 0)
+    lane = lax.broadcasted_iota(jnp.int32, (width, rows.shape[1]), 1)
+    fold = jnp.where(lane % width == row, 1.0, 0.0).astype(jnp.bfloat16)
+    hi, mid, low = thirds(rows)
+    return multiply_rows(jnp.concatenate([fold] * 3, axis=1), jnp.concatenate([low, mid, hi], axis=1))
 
 
 def gram_body(
@@ -95,17 +95,19 @@
     some = seqs // STEPS
     step = pl.program_id(0)
     start = pl.multiple_of(step * some * 8, some * 8)
-    a_part[pl.ds(start, some * 8), :] = project(act_ref, in_ref, some, tokens)
-    g_part[pl.ds(start, some * 8), :] = project(grad_ref, out_ref, some, tokens)
+    for part, x_ref, w_ref in ((a_part, act_ref, in_ref), (g_part, grad_ref, out_ref)):
+        found = project(x_ref, w_ref, some, tokens)
+        for h in range(2):
+            part[h, pl.ds(start, some * 8), :] = found[:, TILE * h : TILE * (h + 1)]
 
     @pl.when(step == STEPS - 1)
     def _():
         live = mask_ref[...].astype(jnp.float32)
         width = in_ref.shape[0]
-        acts = by_token(a_part[...], width, tokens)
-        grads = by_token(g_part[...], out_ref.shape[0], tokens)
-        acts = [acts[:, TILE * t : TILE * t + seqs] for t in range(tokens)]
-        grads = [grads[:, TILE * t : TILE * t + seqs] * live[t : t + 1, :] for t in range(tokens)]
+        acts = [by_token(a_part, width, t, tokens) for t in range(tokens)]
+        grads = [
+            by_token(g_part, out_ref.shape[0], t, tokens) * live[t : t + 1, :] for t in range(tokens)
+        ]
         for g in range(K // width):
             total = grads[0][g : g + 1, :] * acts[0]
             for t in range(1, tokens):
@@ -157,46 +159,84 @@
             jax.ShapeDtypeStruct(half, jnp.float32),
         ),
         scratch_shapes=[
-            pltpu.VMEM((seqs * 8, 2 * TILE), jnp.float32),
-            pltpu.VMEM((seqs * 8, 2 * TILE), jnp.float32),
+            pltpu.VMEM((2, seqs * 8, TILE), jnp.float32),
+            pltpu.VMEM((2, seqs * 8, TILE), jnp.float32),
             pltpu.VMEM((PACKED, TILE, TILE), jnp.float32),
         ],
         name="local_gram",
     )(acts, grads, mask_t, proj_in, proj_out)
 
 
-def invert_factor(src, dst):
+def lanes(tile, start):
+    return [jnp.broadcast_to(tile[:, start + j : start + j + 1], (8, TILE)) for j in range(8)]
+
+
+def across(tile, j):
+    return jnp.broadcast_to(tile[j : j + 1, :], (8, TILE))
+
+
+def reduce_rows(tiles, base):
     lane = lax.broadcasted_iota(jnp.int32, (8, TILE), 1)
     sub = lax.broadcasted_iota(jnp.int32, (8, TILE), 0)
-    groups = TILE // 8
+    tiles = list(tiles)
+    groups = len(tiles)
+    done = []
+    corner = lanes(tiles[0], base)
     for g in range(groups):
-        tiles = [src[8 * q : 8 * q + 8, :] for q in range(g, groups)]
-        cols = [
-            [jnp.broadcast_to(t[:, 8 * g + j : 8 * g + j + 1], (8, TILE)) for t in tiles]
-            for j in range(8)
-        ]
-        inside = (lane >= 8 * g) & (lane < 8 * g + 8)
-        tiles = [jnp.where(inside, 0.0, t) for t in tiles]
-        tiles[0] = jnp.where(lane == sub + 8 * g, 1.0, tiles[0])
+        more = g + 1 < groups
+        at = base + 8 * g
+        below = {q: lanes(tiles[q], at) for q in range(g + 1, groups)}
+        ahead = lanes(tiles[g], at + 8) if more else []
+        following = lanes(tiles[g + 1], at + 8) if more else []
+        inside = (lane >= at) & (lane < at + 8)
+        for q in range(g + 1, groups):
+            tiles[q] = jnp.where(inside, 0.0, tiles[q])
+        top = jnp.where(lane == sub + at, 1.0, jnp.where(inside, 0.0, tiles[g]))
         scale = jnp.zeros((8, TILE), jnp.float32)
         for j in range(8):
-            pivot = jnp.broadcast_to(cols[j][0][j : j + 1, :], (8, TILE))
+            pivot = across(corner[j], j)
             guess = pl.reciprocal(pivot, approx=True)
             fix = 2.0 - pivot * guess
             inverse = guess * fix
-            row = jnp.broadcast_to(tiles[0][j : j + 1, :], (8, TILE))
             root = lax.rsqrt(pivot)
             root = root * (1.5 - 0.5 * (pivot * root) * root)
             scale = jnp.where(sub == j, root, scale)
-            lead = jnp.where(sub > j, cols[j][0] * guess, 0.0) * fix
-            factors = [lead] + [c * inverse for c in cols[j][1:]]
+            lead = jnp.where(sub > j, corner[j] * guess, 0.0) * fix
+            row = across(top, j)
+            top = top - lead * row
+            heads = {l: across(corner[l], j) for l in range(j + 1, 8)}
             for l in range(j + 1, 8):
-                top = jnp.broadcast_to(cols[l][0][j : j + 1, :], (8, TILE))
-                cols[l] = [c - m * top for c, m in zip(cols[l], factors)]
-            tiles = [t - m * row for t, m in zip(tiles, factors)]
-        dst[8 * g : 8 * g + 8, :] = jnp.where(lane <= sub + 8 * g, tiles[0] * scale, 0.0)
-        for q in range(1, len(tiles)):
-            src[8 * (g + q) : 8 * (g + q) + 8, :] = tiles[q]
+                corner[l] = corner[l] - lead * heads[l]
+            coming = [across(c, j) for c in ahead]
+            ahead = [c - lead * r for c, r in zip(ahead, coming)]
+            for q in range(g + 1, groups):
+                factor = below[q][j] * inverse
+                for l in range(j + 1, 8):
+                    below[q][l] = below[q][l] - factor * heads[l]
+                if q == g + 1:
+                    following = [c - factor * r for c, r in zip(following, coming)]
+                tiles[q] = tiles[q] - factor * row
+        done.append(top * scale)
+        corner = following
+    return jnp.concatenate(done, axis=0)
+
+
+def invert_factor(src, dst):
+    half = TILE // 2
+    row = lax.broadcasted_iota(jnp.int32, (half, TILE), 0)
+    lane = lax.broadcasted_iota(jnp.int32, (half, TILE), 1)
+    upper = reduce_rows([src[8 * q : 8 * q + 8, :] for q in range(half // 8)], 0)
+    kept = jnp.where((lane > row) & (lane < half), 0.0, upper)
+    dst[:half, :] = jnp.where(lane < half, kept, 0.0)
+    product = lax.dot_general(
+        left_parts(thirds(upper), 0),
+        right_parts(thirds(kept), 0),
+        (((0,), (0,)), ((), ())),
+        preferred_element_type=jnp.float32,
+    )[half:, :]
+    lower = jnp.where(lane < half, 0.0, src[half:, :]) - product
+    lower = reduce_rows([lower[8 * q : 8 * q + 8, :] for q in range(half // 8)], half)
+    dst[half:, :] = jnp.where(lane <= row + half, lower, 0.0)
 
 
 def solve_body(

time: 134 us -> 125 us (0.933)
  Pallas kernels: 56.3 us -> 46.1 us
    pallas_call x1, Pallas kernels: 45.5 us -> 36.3 us  [damped_scores(): pl.pallas_call(solve_body, in_specs=[vmem] * 5, out_shape=jax.ShapeDtypeS...]
  transfers between devices with their start and end apart: 3 -> 3, of which waited for: 2 -> 3; matrix products, arithmetic and copies ran while one was open for 0% -> 0% of each run, Pallas kernels for 8% -> 8%
where the time goes in v4:
time: 125 us
  blocking collectives  61.5 us (49%)
  Pallas kernels  46.1 us (37%)
  starting transfers between devices  8.22 us (7%)
  waiting for transfers between devices  6.21 us (5%)
  other arithmetic  1.51 us (1%)
    pallas_call x1, Pallas kernels, damped_scores(): pl.pallas_call(solve_body, in_specs=[vmem] * 5, out_shape=jax.ShapeDtypeS...  36.3 us
    all_to_all x2, blocking collectives, gather_rows(): return lax.all_to_all(copies, axes, 0, 0, tiled=True).reshape(-1, TILE)  35 us
    all_to_all x1, blocking collectives, scatter_sum(): return jnp.sum(lax.all_to_all(pieces, axes, 0, 0, tiled=True), axis=0)  26.5 us
    pallas_call x1, Pallas kernels, local_gram(): pl.pallas_call(gram_body, grid=(STEPS,), in_specs=[pl.BlockSpec((acts.sha...  9.87 us
    ppermute x1, starting transfers between devices, summed(): return (mine, lax.ppermute(mine, 'core', SWAP))  3.6 us
    ppermute x1, waiting for transfers between devices, summed(): rows = (kept + lax.ppermute(sent, 'core', SWAP)).reshape(-1, TILE)  2.68 us
  transfers between devices with their start and end apart: 3, of which 3 were waited for; matrix products, arithmetic and copies ran while one was open for 0% of the time, Pallas kernels for 8%

profile of v4, /device:TPU:1, one launch (start us, length us, event | category | flops | bytes accessed | tf_op | source)
XLA Modules:
  0.0 124.8 jit_solution(205700192659361419)
XLA Ops:
  0.0 2.5 %collective-permute-start = (f32[128,1024]{1,0:T(8,128)}, f32[128,1024]{1,0:T(8,128)S(1)}, u32[]{:S(2)}, u32[]{:S(2)}) collective-permute-start(f32[128,1024]{1,0:T(8,128)} %query_ref.1), channel_id=1, source_target_pairs={{0,1},{1,0},{2,3},{3,2},{4,5},{5,4},{6,7},{7,6},{8,9},{9,8},{10,11... | collective-permute-start | bytes 1572872 | tf_op jit(solution)/shard_map/ppermute | solution.py:348
  2.5 9.9 %local_gram.1 = (f32[1024,64]{1,0:T(8,128)}, f32[18,128,128]{2,1,0:T(8,128)}, f32[18,128,128]{2,1,0:T(8,128)}) custom-call(bf16[28672,128]{1,0:T(8,128)(2,1)} %bitcast.13, bf16[8192,128]{1,0:T(8,128)(2,1)} %bitcast.17, s32[4,64]{1,0:T(4,128)} %bitcast.18, bf16[32,14336]{1,0:T(8,128)(2,1)} %in_ref.1, bf16[32,4096]{1,0:T(8,128)(2,1)} %out_ref.1), custom_call_target="tpu_custom_call" | custom-call | tf_op jit(solution)/shard_map/local_gram/pallas_call | solution.py:145
  12.3 1.1 collective-permute-done.query2_ref
  13.4 0.0 copy-start.2
  13.4 2.2 %collective-permute-start.1 = (f32[18,128,128]{2,1,0:T(8,128)}, f32[18,128,128]{2,1,0:T(8,128)S(1)}, u32[]{:S(2)}, u32[]{:S(2)}) collective-permute-start(f32[18,128,128]{2,1,0:T(8,128)} %get-tuple-element.14), channel_id=1, source_target_pairs={{0,2},{2,0},{1,3},{3,1},{4,6},{6,4},{5,7},{7,5},{8,10},{10,8},{9,1... | collective-permute-start | bytes 3538952 | tf_op jit(solution)/shard_map/ppermute | solution.py:339
  15.5 2.7 %collective-permute-done.1 = f32[18,128,128]{2,1,0:T(8,128)S(1)} collective-permute-done((f32[18,128,128]{2,1,0:T(8,128)}, f32[18,128,128]{2,1,0:T(8,128)S(1)}, u32[]{:S(2)}, u32[]{:S(2)}) %collective-permute-start.1) | collective-permute-done | bytes 1179680 | tf_op jit(solution)/shard_map/ppermute | solution.py:339
  18.2 1.4 %add.3 = f32[18,128,128]{2,1,0:T(8,128)S(1)} add(f32[18,128,128]{2,1,0:T(8,128)} %get-tuple-element.13, f32[18,128,128]{2,1,0:T(8,128)S(1)} %collective-permute-done.1) | non-fusion elementwise | flops 294912 | bytes 3538944 | tf_op jit(solution)/shard_map/add | solution.py:339
  19.7 0.0 copy-done.2
  19.7 26.5 %all_to_all.15 = f32[32,72,128]{2,1,0:T(8,128)S(1)} all-to-all(f32[32,72,128]{2,1,0:T(8,128)S(1)} %bitcast.14), channel_id=1, replica_groups=mesh['z_hi'=4,'x'=4,'y'=4,'core'=2,'z_lo'=2] {'x','y','z_lo'}, dimensions={0} | all-to-all | bytes 2359296 | tf_op jit(solution)/shard_map/all_to_all | solution.py:329
  46.1 0.1 reduce_sum.18
  46.2 15.0 %all_to_all.16 = f32[4,72,128]{2,1,0:T(8,128)S(1)} all-to-all(f32[4,72,128]{2,1,0:T(8,128)S(1)} %broadcast_in_dim.4), channel_id=1, replica_groups=mesh['z_hi'=4,'x'=4,'y'=4,'core'=2,'z_lo'=2] {'z_hi'}, dimensions={0} | all-to-all | bytes 294912 | tf_op jit(solution)/shard_map/all_to_all | solution.py:335
  61.2 0.1 broadcast_in_dim.5
  61.3 20.1 %all_to_all.17 = f32[32,72,128]{2,1,0:T(8,128)S(1)} all-to-all(f32[32,72,128]{2,1,0:T(8,128)S(1)} %broadcast_in_dim.5), channel_id=1, replica_groups=mesh['z_hi'=4,'x'=4,'y'=4,'core'=2,'z_lo'=2] {'x','y','z_lo'}, dimensions={0} | all-to-all | bytes 2359296 | tf_op jit(solution)/shard_map/all_to_all | solution.py:335
  81.4 0.0 copy-start
  81.4 3.6 %collective-permute-start.2 = (f32[18,128,128]{2,1,0:T(8,128)S(1)}, f32[18,128,128]{2,1,0:T(8,128)S(1)}, u32[]{:S(2)}, u32[]{:S(2)}) collective-permute-start(f32[18,128,128]{2,1,0:T(8,128)S(1)} %bitcast.15), channel_id=1, source_target_pairs={{0,2},{2,0},{1,3},{3,1},{4,6},{6,4},{5,7},{7,5},{8,10},{10,8},{9,1... | collective-permute-start | bytes 3538952 | tf_op jit(solution)/shard_map/ppermute | solution.py:344
  85.0 2.5 %collective-permute-done.2.other_ref = f32[18,128,128]{2,1,0:T(8,128)S(1)} collective-permute-done((f32[18,128,128]{2,1,0:T(8,128)S(1)}, f32[18,128,128]{2,1,0:T(8,128)S(1)}, u32[]{:S(2)}, u32[]{:S(2)}) %collective-permute-start.2) | collective-permute-done | bytes 1179680 | tf_op jit(solution)/shard_map/ppermute | solution.py:344
  87.4 0.0 copy-start.1
  87.4 0.0 copy-done
  87.4 1.1 copy-done.1
  88.5 36.3 %damped_scores.1 = f32[64,256]{1,0:T(8,128)} custom-call(f32[18,128,128]{2,1,0:T(8,128)} %bitcast.16, f32[18,128,128]{2,1,0:T(8,128)} %copy-done.1, f32[128,1024]{1,0:T(8,128)} %query_ref.1, f32[128,1024]{1,0:T(8,128)} %copy-done.2, f32[1024,64]{1,0:T(8,128)} %get-tuple-element.16.outer_ref), custom_call_target="tpu_custom_call" | custom-call | tf_op jit(solution)/shard_map/damped_scores/pallas_call | solution.py:305
  (2 shorter events, 0.0 us)
Async XLA Ops:
  0.0 13.4 %collective-permute-start = (f32[128,1024]{1,0:T(8,128)}, f32[128,1024]{1,0:T(8,128)S(1)}, u32[]{:S(2)}, u32[]{:S(2)}) collective-permute-start(f32[128,1024]{1,0:T(8,128)} %query_ref.1), channel_id=1, source_target_pairs={{0,1},{1,0},{2,3},{3,2},{4,5},{5,4},{6,7},{7,6},{8,9},{9,8},{10,11... | collective-permute-start | bytes 1572872 | tf_op jit(solution)/shard_map/ppermute | solution.py:348
  13.4 6.3 %copy-start.2 = (f32[128,1024]{1,0:T(8,128)}, f32[128,1024]{1,0:T(8,128)S(1)}, u32[]{:S(2)}) copy-start(f32[128,1024]{1,0:T(8,128)S(1)} %collective-permute-done.query2_ref) | copy-start | bytes 1572868
  13.4 4.8 %collective-permute-start.1 = (f32[18,128,128]{2,1,0:T(8,128)}, f32[18,128,128]{2,1,0:T(8,128)S(1)}, u32[]{:S(2)}, u32[]{:S(2)}) collective-permute-start(f32[18,128,128]{2,1,0:T(8,128)} %get-tuple-element.14), channel_id=1, source_target_pairs={{0,2},{2,0},{1,3},{3,1},{4,6},{6,4},{5,7},{7,5},{8,10},{10,8},{9,1... | collective-permute-start | bytes 3538952 | tf_op jit(solution)/shard_map/ppermute | solution.py:339
  81.4 6.1 %copy-start = (f32[32,72,128]{2,1,0:T(8,128)}, f32[32,72,128]{2,1,0:T(8,128)S(1)}, u32[]{:S(2)}) copy-start(f32[32,72,128]{2,1,0:T(8,128)S(1)} %all_to_all.17) | copy-start | bytes 3538948
  81.4 6.1 %collective-permute-start.2 = (f32[18,128,128]{2,1,0:T(8,128)S(1)}, f32[18,128,128]{2,1,0:T(8,128)S(1)}, u32[]{:S(2)}, u32[]{:S(2)}) collective-permute-start(f32[18,128,128]{2,1,0:T(8,128)S(1)} %bitcast.15), channel_id=1, source_target_pairs={{0,2},{2,0},{1,3},{3,1},{4,6},{6,4},{5,7},{7,5},{8,10},{10,8},{9,1... | collective-permute-start | bytes 3538952 | tf_op jit(solution)/shard_map/ppermute | solution.py:344
  87.4 1.1 copy-start.1

commit v5 on v4

--- a/solution.py
+++ b/solution.py
@@ -7,6 +7,7 @@
 from jax.experimental.pallas import tpu as pltpu
 from jax.sharding import Mesh
 from jax.sharding import PartitionSpec as P
+
 
 K = 1024
 TILE = 128
@@ -335,20 +336,26 @@
     return lax.all_to_all(copies, axes, 0, 0, tiled=True).reshape(-1, TILE)
 
 
-def summed(kept, sent):
-    rows = (kept + lax.ppermute(sent, "core", SWAP)).reshape(-1, TILE)
-    rows = scatter_sum(rows, NEAR)
-    everyone = gather_rows(rows, ("z_hi",)).reshape(SIZES["z_hi"], -1, TILE)
-    rows = gather_rows(jnp.sum(everyone, axis=0), NEAR)
-    mine = rows.reshape(kept.shape)
+def exchange_sum(rows):
+    peers = SIZES["z_hi"]
+    one, two, three = (
+        lax.ppermute(rows, "z_hi", [(a, a ^ d) for a in range(peers)]) for d in range(1, peers)
+    )
+    return (rows + one) + (two + three)
+
+
+def summed(rows, shape):
+    rows = exchange_sum(scatter_sum(rows.reshape(-1, TILE), NEAR))
+    mine = gather_rows(rows, NEAR).reshape(shape)
     return mine, lax.ppermute(mine, "core", SWAP)
 
 
 def on_device(hidden_acts, out_grads, loss_mask, proj_in, proj_out, queries):
     other_queries = lax.ppermute(queries, "z_lo", SWAP)
     outer_t, kept, sent = local_gram(hidden_acts, out_grads, loss_mask.T, proj_in, proj_out)
-    other_queries, kept, sent = lax.optimization_barrier((other_queries, kept, sent))
-    mine, other = summed(kept, sent)
+    both = kept + lax.ppermute(sent, "core", SWAP)
+    other_queries, both = lax.optimization_barrier((other_queries, both))
+    mine, other = summed(both, kept.shape)
     return damped_scores(mine, other, queries, other_queries, outer_t)
 
 

time: 125 us -> 128 us (1.024)
  blocking collectives: 61.5 us -> 45.2 us
  waiting for transfers between devices: 6.21 us -> 19.3 us
  starting transfers between devices: 8.22 us -> 14.2 us
    all_to_all x2 -> x1, blocking collectives: 35 us -> 20.8 us  [gather_rows(): return lax.all_to_all(copies, axes, 0, 0, tiled=True).reshape(-1, TILE)]
    ppermute x1 -> x4, starting transfers between devices: 2.16 us -> 10.5 us  [the longest x3 7.29 us: exchange_sum(): lax.ppermute(rows, 'z_hi', [(a, a ^ d) for a in range(peers)])]
    ppermute x1, waiting for transfers between devices: 1.05 us -> 9.28 us  [on_device(): other_queries = lax.ppermute(queries, 'z_lo', SWAP)]
    ppermute x1 -> x4, waiting for transfers between devices: 2.68 us -> 7.59 us  [the longest x3 4.91 us: exchange_sum(): lax.ppermute(rows, 'z_hi', [(a, a ^ d) for a in range(peers)])]
    ppermute x1, starting transfers between devices: 2.46 us -> 0.01 us  [on_device(): other_queries = lax.ppermute(queries, 'z_lo', SWAP)]
    all_to_all x1, blocking collectives: 26.5 us -> 24.4 us  [scatter_sum(): return jnp.sum(lax.all_to_all(pieces, axes, 0, 0, tiled=True), axis=0)]
  transfers between devices with their start and end apart: 3 -> 6, of which waited for: 3 -> 5; matrix products, arithmetic and copies ran while one was open for 0% -> 1% of each run, Pallas kernels for 8% -> 0%
where the time goes in v5:
time: 128 us
  Pallas kernels  46.2 us (36%)
  blocking collectives  45.2 us (35%)
  waiting for transfers between devices  19.3 us (15%)
  starting transfers between devices  14.2 us (11%)
  other arithmetic  1.51 us (1%)
    pallas_call x1, Pallas kernels, damped_scores(): pl.pallas_call(solve_body, in_specs=[vmem] * 5, out_shape=jax.ShapeDtypeS...  36.3 us
    all_to_all x1, blocking collectives, scatter_sum(): return jnp.sum(lax.all_to_all(pieces, axes, 0, 0, tiled=True), axis=0)  24.4 us
    all_to_all x1, blocking collectives, gather_rows(): return lax.all_to_all(copies, axes, 0, 0, tiled=True).reshape(-1, TILE)  20.8 us
    pallas_call x1, Pallas kernels, local_gram(): pl.pallas_call(gram_body, grid=(STEPS,), in_specs=[pl.BlockSpec((acts.sha...  9.96 us
    ppermute x1, waiting for transfers between devices, on_device(): other_queries = lax.ppermute(queries, 'z_lo', SWAP)  9.28 us
    ppermute x3, starting transfers between devices, exchange_sum(): lax.ppermute(rows, 'z_hi', [(a, a ^ d) for a in range(peers)])  7.29 us
    ppermute x3, waiting for transfers between devices, exchange_sum(): lax.ppermute(rows, 'z_hi', [(a, a ^ d) for a in range(peers)])  4.91 us
    ppermute x1, starting transfers between devices, summed(): return (mine, lax.ppermute(mine, 'core', SWAP))  3.67 us
  transfers between devices with their start and end apart: 6, of which 5 were waited for; matrix products, arithmetic and copies ran while one was open for 1% of the time, Pallas kernels for 0%

profile of v5, /device:TPU:1, one launch (start us, length us, event | category | flops | bytes accessed | tf_op | source)
XLA Modules:
  0.0 127.6 jit_solution(14562869655263835772)
XLA Ops:
  0.0 0.0 copy-start.2
  0.0 10.0 %local_gram.1 = (f32[1024,64]{1,0:T(8,128)}, f32[18,128,128]{2,1,0:T(8,128)}, f32[18,128,128]{2,1,0:T(8,128)}) custom-call(bf16[28672,128]{1,0:T(8,128)(2,1)} %bitcast.13, bf16[8192,128]{1,0:T(8,128)(2,1)} %bitcast.17, s32[4,64]{1,0:T(4,128)} %bitcast.18, bf16[32,14336]{1,0:T(8,128)(2,1)} %in_ref.1, bf16[32,4096]{1,0:T(8,128)(2,1)} %out_ref.1), custom_call_target="tpu_custom_call" | custom-call | tf_op jit(solution)/shard_map/local_gram/pallas_call | solution.py:146
  10.0 3.2 %collective-permute-start.1 = (f32[18,128,128]{2,1,0:T(8,128)}, f32[18,128,128]{2,1,0:T(8,128)S(1)}, u32[]{:S(2)}, u32[]{:S(2)}) collective-permute-start(f32[18,128,128]{2,1,0:T(8,128)} %get-tuple-element.11), channel_id=1, source_target_pairs={{0,2},{2,0},{1,3},{3,1},{4,6},{6,4},{5,7},{7,5},{8,10},{10,8},{9,1... | collective-permute-start | bytes 3538952 | tf_op jit(solution)/shard_map/ppermute | solution.py:356
  13.1 0.0 copy-done.2
  13.2 0.0 collective-permute-start
  13.2 2.7 %collective-permute-done.1 = f32[18,128,128]{2,1,0:T(8,128)S(1)} collective-permute-done((f32[18,128,128]{2,1,0:T(8,128)}, f32[18,128,128]{2,1,0:T(8,128)S(1)}, u32[]{:S(2)}, u32[]{:S(2)}) %collective-permute-start.1) | collective-permute-done | bytes 1179680 | tf_op jit(solution)/shard_map/ppermute | solution.py:356
  15.8 1.4 %add.12 = f32[18,128,128]{2,1,0:T(8,128)S(1)} add(f32[18,128,128]{2,1,0:T(8,128)} %get-tuple-element.10, f32[18,128,128]{2,1,0:T(8,128)S(1)} %collective-permute-done.1) | non-fusion elementwise | flops 294912 | bytes 3538944 | tf_op jit(solution)/shard_map/add | solution.py:356
  17.3 9.3 %collective-permute-done.query2_ref = f32[128,1024]{1,0:T(8,128)S(1)} collective-permute-done((f32[128,1024]{1,0:T(8,128)S(1)}, f32[128,1024]{1,0:T(8,128)S(1)}, u32[]{:S(2)}, u32[]{:S(2)}) %collective-permute-start) | collective-permute-done | bytes 524320 | tf_op jit(solution)/shard_map/ppermute | solution.py:354
  26.5 0.0 copy-start.3
  26.5 24.4 %all_to_all.10 = f32[32,72,128]{2,1,0:T(8,128)S(1)} all-to-all(f32[32,72,128]{2,1,0:T(8,128)S(1)} %bitcast.14), channel_id=1, replica_groups=mesh['z_hi'=4,'x'=4,'y'=4,'core'=2,'z_lo'=2] {'x','y','z_lo'}, dimensions={0} | all-to-all | bytes 2359296 | tf_op jit(solution)/shard_map/all_to_all | solution.py:330
  51.0 0.0 copy-done.3
  51.0 0.1 reduce_sum.9
  51.0 3.1 %collective-permute-start.2 = (f32[72,128]{1,0:T(8,128)S(1)}, f32[72,128]{1,0:T(8,128)S(1)}, u32[]{:S(2)}, u32[]{:S(2)}) collective-permute-start(f32[72,128]{1,0:T(8,128)S(1)} %reduce_sum.9), channel_id=1, source_target_pairs={{0,64},{64,0},{128,192},{192,128},{1,65},{65,1},{129,193},{193,129... | collective-permute-start | bytes 110600 | tf_op jit(solution)/shard_map/ppermute | solution.py:342
  54.1 4.2 %collective-permute-start.3 = (f32[72,128]{1,0:T(8,128)S(1)}, f32[72,128]{1,0:T(8,128)S(1)}, u32[]{:S(2)}, u32[]{:S(2)}) collective-permute-start(f32[72,128]{1,0:T(8,128)S(1)} %reduce_sum.9), channel_id=1, source_target_pairs={{0,128},{64,192},{128,0},{192,64},{1,129},{65,193},{129,1},{193,65... | collective-permute-start | bytes 110600 | tf_op jit(solution)/shard_map/ppermute | solution.py:342
  58.3 0.0 collective-permute-start.4
  58.3 0.0 collective-permute-done.2
  58.3 2.5 %collective-permute-done.3 = f32[72,128]{1,0:T(8,128)S(1)} collective-permute-done((f32[72,128]{1,0:T(8,128)S(1)}, f32[72,128]{1,0:T(8,128)S(1)}, u32[]{:S(2)}, u32[]{:S(2)}) %collective-permute-start.3) | collective-permute-done | bytes 36896 | tf_op jit(solution)/shard_map/ppermute | solution.py:342
  60.8 2.4 %collective-permute-done.4 = f32[72,128]{1,0:T(8,128)S(1)} collective-permute-done((f32[72,128]{1,0:T(8,128)S(1)}, f32[72,128]{1,0:T(8,128)S(1)}, u32[]{:S(2)}, u32[]{:S(2)}) %collective-permute-start.4) | collective-permute-done | bytes 36896 | tf_op jit(solution)/shard_map/ppermute | solution.py:342
  63.2 0.1 broadcast_in_dim.2
  63.3 20.8 %all_to_all.11 = f32[32,72,128]{2,1,0:T(8,128)S(1)} all-to-all(f32[32,72,128]{2,1,0:T(8,128)S(1)} %broadcast_in_dim.2), channel_id=1, replica_groups=mesh['z_hi'=4,'x'=4,'y'=4,'core'=2,'z_lo'=2] {'x','y','z_lo'}, dimensions={0} | all-to-all | bytes 2359296 | tf_op jit(solution)/shard_map/all_to_all | solution.py:336
  84.2 0.0 copy-start
  84.2 3.7 %collective-permute-start.5 = (f32[18,128,128]{2,1,0:T(8,128)S(1)}, f32[18,128,128]{2,1,0:T(8,128)S(1)}, u32[]{:S(2)}, u32[]{:S(2)}) collective-permute-start(f32[18,128,128]{2,1,0:T(8,128)S(1)} %bitcast.15), channel_id=1, source_target_pairs={{0,2},{2,0},{1,3},{3,1},{4,6},{6,4},{5,7},{7,5},{8,10},{10,8},{9,1... | collective-permute-start | bytes 3538952 | tf_op jit(solution)/shard_map/ppermute | solution.py:350
  87.8 2.5 %collective-permute-done.5.other_ref = f32[18,128,128]{2,1,0:T(8,128)S(1)} collective-permute-done((f32[18,128,128]{2,1,0:T(8,128)S(1)}, f32[18,128,128]{2,1,0:T(8,128)S(1)}, u32[]{:S(2)}, u32[]{:S(2)}) %collective-permute-start.5) | collective-permute-done | bytes 1179680 | tf_op jit(solution)/shard_map/ppermute | solution.py:350
  90.3 0.0 copy-start.1
  90.3 0.0 copy-done
  90.3 1.0 copy-done.1
  91.4 36.3 %damped_scores.1 = f32[64,256]{1,0:T(8,128)} custom-call(f32[18,128,128]{2,1,0:T(8,128)} %bitcast.16, f32[18,128,128]{2,1,0:T(8,128)} %copy-done.1, f32[128,1024]{1,0:T(8,128)} %query_ref.1, f32[128,1024]{1,0:T(8,128)} %copy-done.3, f32[1024,64]{1,0:T(8,128)} %get-tuple-element.14.outer_ref), custom_call_target="tpu_custom_call" | custom-call | tf_op jit(solution)/shard_map/damped_scores/pallas_call | solution.py:306
  (1 shorter events, 0.0 us)
Async XLA Ops:
  0.0 13.1 %copy-start.2 = (f32[128,1024]{1,0:T(8,128)S(1)}, f32[128,1024]{1,0:T(8,128)}, u32[]{:S(2)}) copy-start(f32[128,1024]{1,0:T(8,128)} %query_ref.1) | copy-start | bytes 1572868
  10.0 5.9 %collective-permute-start.1 = (f32[18,128,128]{2,1,0:T(8,128)}, f32[18,128,128]{2,1,0:T(8,128)S(1)}, u32[]{:S(2)}, u32[]{:S(2)}) collective-permute-start(f32[18,128,128]{2,1,0:T(8,128)} %get-tuple-element.11), channel_id=1, source_target_pairs={{0,2},{2,0},{1,3},{3,1},{4,6},{6,4},{5,7},{7,5},{8,10},{10,8},{9,1... | collective-permute-start | bytes 3538952 | tf_op jit(solution)/shard_map/ppermute | solution.py:356
  13.2 13.4 %collective-permute-start = (f32[128,1024]{1,0:T(8,128)S(1)}, f32[128,1024]{1,0:T(8,128)S(1)}, u32[]{:S(2)}, u32[]{:S(2)}) collective-permute-start(f32[128,1024]{1,0:T(8,128)S(1)} %copy-done.2), channel_id=1, source_target_pairs={{0,1},{1,0},{2,3},{3,2},{4,5},{5,4},{6,7},{7,6},{8,9},{9,8},{10,11... | collective-permute-start | bytes 1572872 | tf_op jit(solution)/shard_map/ppermute | solution.py:354
  26.5 24.4 %copy-start.3 = (f32[128,1024]{1,0:T(8,128)}, f32[128,1024]{1,0:T(8,128)S(1)}, u32[]{:S(2)}) copy-start(f32[128,1024]{1,0:T(8,128)S(1)} %collective-permute-done.query2_ref) | copy-start | bytes 1572868
  51.0 7.3 %collective-permute-start.2 = (f32[72,128]{1,0:T(8,128)S(1)}, f32[72,128]{1,0:T(8,128)S(1)}, u32[]{:S(2)}, u32[]{:S(2)}) collective-permute-start(f32[72,128]{1,0:T(8,128)S(1)} %reduce_sum.9), channel_id=1, source_target_pairs={{0,64},{64,0},{128,192},{192,128},{1,65},{65,1},{129,193},{193,129... | collective-permute-start | bytes 110600 | tf_op jit(solution)/shard_map/ppermute | solution.py:342
  54.1 6.7 %collective-permute-start.3 = (f32[72,128]{1,0:T(8,128)S(1)}, f32[72,128]{1,0:T(8,128)S(1)}, u32[]{:S(2)}, u32[]{:S(2)}) collective-permute-start(f32[72,128]{1,0:T(8,128)S(1)} %reduce_sum.9), channel_id=1, source_target_pairs={{0,128},{64,192},{128,0},{192,64},{1,129},{65,193},{129,1},{193,65... | collective-permute-start | bytes 110600 | tf_op jit(solution)/shard_map/ppermute | solution.py:342
  58.3 4.9 %collective-permute-start.4 = (f32[72,128]{1,0:T(8,128)S(1)}, f32[72,128]{1,0:T(8,128)S(1)}, u32[]{:S(2)}, u32[]{:S(2)}) collective-permute-start(f32[72,128]{1,0:T(8,128)S(1)} %reduce_sum.9), channel_id=1, source_target_pairs={{0,192},{64,128},{128,64},{192,0},{1,193},{65,129},{129,65},{193,1... | collective-permute-start | bytes 110600 | tf_op jit(solution)/shard_map/ppermute | solution.py:342
  84.2 6.2 %copy-start = (f32[32,72,128]{2,1,0:T(8,128)}, f32[32,72,128]{2,1,0:T(8,128)S(1)}, u32[]{:S(2)}) copy-start(f32[32,72,128]{2,1,0:T(8,128)S(1)} %all_to_all.11) | copy-start | bytes 3538948
  84.2 6.1 %collective-permute-start.5 = (f32[18,128,128]{2,1,0:T(8,128)S(1)}, f32[18,128,128]{2,1,0:T(8,128)S(1)}, u32[]{:S(2)}, u32[]{:S(2)}) collective-permute-start(f32[18,128,128]{2,1,0:T(8,128)S(1)} %bitcast.15), channel_id=1, source_target_pairs={{0,2},{2,0},{1,3},{3,1},{4,6},{6,4},{5,7},{7,5},{8,10},{10,8},{9,1... | collective-permute-start | bytes 3538952 | tf_op jit(solution)/shard_map/ppermute | solution.py:350
  90.3 1.0 copy-start.1
